TPU v7x, 128 devices: a whole 4x4x4 slice. The times are simulated.
128 devices in a mesh: wide: 8 (over z, core), blk: 16 (over y, x).
Axes of the slice: x: 4, y: 4, z: 4, core: 2. Of those that a mesh axis runs over, the one named last changes fastest.
Arguments:
- rhs: float32 [524288, 256], P(('wide', 'blk'))
- near_blocks: bfloat16 [524288, 1536], P(('wide', 'blk')), may hold values from -0.078125 to 0.078125
- source_basis: bfloat16 [524288, 64], P(('wide', 'blk')), may hold values from -0.5 to 0.5
- target_basis: bfloat16 [524288, 64], P(('wide', 'blk')), may hold values from -0.375 to 0.375
- far_coupling: bfloat16 [4096, 4, 64, 64], P(('wide', 'blk')), may hold values from -0.375 to 0.375
- send_ids: int32 [128, 128, 1], P(('wide', 'blk')), may hold values from 0 to 31
- far_list: int32 [128, 128], P(('wide', 'blk')), may hold values from 0 to 127, each once within a row
Outputs:
- solution: float32 [524288, 256], P(('wide', 'blk'))
- residual: float32 [524288, 256], P(('wide', 'blk'))
Inputs may be any that keep to these rules, and one draw needn't show every extreme that they name: Each row of far_list names each received slot 0 to 127 exactly once.
All inputs are finite; a program needn't handle non-finite values.
Results may differ from a plain program's by a relative error of at most 0.0035.
The roundings to bfloat16 on the way count: a program that leaves them out, or rounds other values in their place, can miss the bound.
Values may be sent and summed in bfloat16 or wider, within the bound.
No kernel may reach another device: no remote copies, remote signals or barrier semaphores. Data moves between devices by JAX's collectives and lax.ppermute only.
A program may use at most 128 MiB of HBM per device.

v0:
```python
import jax
import jax.numpy as jnp
from jax import lax
from jax.sharding import Mesh
from jax.sharding import PartitionSpec as P

NEAR = 1024
HALO = 256
LEAF = 128
ITERS = 2
BLK = ("blk_0", "blk_1")
WIDE_BLK = ("wide_0", "wide_1", "blk_0", "blk_1")


def with_halo(value, sides, width):
    for axis, dim in sides:
        count, length = (lax.axis_size(axis), value.shape[dim])
        up = [(i, (i + 1) % count) for i in range(count)]
        down = [(j, i) for i, j in up]
        last = lax.slice_in_dim(value, length - width, length, axis=dim)
        first = lax.slice_in_dim(value, 0, width, axis=dim)
        before = lax.ppermute(last, axis, up)
        after = lax.ppermute(first, axis, down)
        value = jnp.concatenate([before, value, after], axis=dim)
    return value


def split_up(value, dim, count):
    before, after = (value.shape[:dim], value.shape[dim + 1 :])
    return jnp.moveaxis(value.reshape(*before, count, -1, *after), dim, 0)


def summed_on_arrival(value, axis, dim):
    parts = split_up(value, dim, lax.axis_size(axis))
    arrived = lax.all_to_all(parts, axis, split_axis=0, concat_axis=0, tiled=True)
    return arrived.sum(axis=0)


def sum_by_axis(value, axes, dim):
    far, near = axes
    parts = split_up(value, dim, lax.axis_size(far))
    nearer = summed_on_arrival(parts, near, dim + 1)
    arrived = lax.all_to_all(nearer, far, split_axis=0, concat_axis=0, tiled=True)
    return arrived.sum(axis=0)


def filled_up(lines, count):
    spare = -lines.shape[0] % count
    if not spare:
        return lines
    return jnp.concatenate([lines, jnp.zeros((spare, *lines.shape[1:]), lines.dtype)])


def copy_for_each(value, axis):
    count = lax.axis_size(axis)
    return lax.all_to_all(
        jnp.broadcast_to(value[None], (count, *value.shape)), axis, 0, 0, tiled=True
    )


def in_order(parts, dim):
    lengths = list(parts.shape[1:])
    lengths[dim] *= parts.shape[0]
    return jnp.moveaxis(parts, 0, dim).reshape(lengths)


def gathered_by_axis(value, axes, dim):
    far, near = axes
    parts = copy_for_each(copy_for_each(value, far), near)
    return in_order(parts.swapaxes(0, 1).reshape(-1, *value.shape), dim)


def total_of(value, axes):
    lines = value.reshape(-1, value.shape[-1])
    own = sum_by_axis(filled_up(lines, lax.axis_size(axes[0]) * lax.axis_size(axes[1])), axes, 0)
    whole = gathered_by_axis(own, axes, 0)
    return whole[: len(lines)].reshape(value.shape)


def near_apply(near_rows, ext):
    outs = []
    for j in range(near_rows.shape[0] // NEAR):
        outs.append(
            jnp.dot(
                near_rows[j * NEAR : (j + 1) * NEAR],
                ext[j * NEAR : j * NEAR + NEAR + 2 * HALO],
                preferred_element_type=jnp.float32,
            )
        )
    return jnp.concatenate(outs, axis=0)


def shards(rhs, near_blocks, source_basis, target_basis, far_coupling, send_ids, far_list):
    rows, width = rhs.shape
    rank = source_basis.shape[1]
    leaves = rows // LEAF
    fanout = far_list.shape[1] // leaves
    senders = send_ids[0].reshape(-1)
    readers = far_list[0]
    source_leaf = source_basis.reshape(leaves, LEAF, rank)
    target_leaf = target_basis.reshape(leaves, LEAF, rank)
    solution = jnp.zeros_like(rhs)
    residual = rhs
    for step in range(ITERS):
        vb = residual.astype(jnp.bfloat16)
        ext = with_halo(vb, ((BLK, 0),), HALO)
        coef = jnp.einsum(
            "lia,lis->las",
            source_leaf,
            vb.reshape(leaves, LEAF, width),
            preferred_element_type=jnp.float32,
        ).astype(jnp.bfloat16)
        outgoing = coef[senders]
        incoming = lax.all_to_all(outgoing, WIDE_BLK, split_axis=0, concat_axis=0, tiled=True)
        near = near_apply(near_blocks, ext)
        picked = incoming[readers].reshape(leaves, fanout, rank, width)
        trans = jnp.einsum(
            "lfab,lfbs->las", far_coupling, picked, preferred_element_type=jnp.float32
        ).astype(jnp.bfloat16)
        far = jnp.einsum(
            "lia,las->lis", target_leaf, trans, preferred_element_type=jnp.float32
        ).reshape(rows, width)
        image = residual + near + far
        local_gram = jnp.einsum("rs,rt->st", image, image, precision=lax.Precision.HIGHEST)
        local_proj = jnp.einsum("rs,rt->st", image, residual, precision=lax.Precision.HIGHEST)
        gram, proj = (
            total_of(local_gram, (("wide_0", "wide_1", "blk_0"), "blk_1")),
            total_of(local_proj, (("wide_0", "wide_1", "blk_0"), "blk_1")),
        )
        factor = jnp.linalg.cholesky(gram)
        alpha = jax.scipy.linalg.cho_solve((factor, True), proj)
        solution = solution + jnp.dot(residual, alpha, precision=lax.Precision.HIGHEST)
        residual = residual - jnp.dot(image, alpha, precision=lax.Precision.HIGHEST)
    return (solution, residual)


def solution(mesh):
    split = Mesh(mesh.devices.reshape(4, 2, 4, 4), ("wide_0", "wide_1", "blk_0", "blk_1"))
    return jax.shard_map(
        shards,
        mesh=split,
        in_specs=(
            P(WIDE_BLK, None),
            P(WIDE_BLK, None),
            P(WIDE_BLK, None),
            P(WIDE_BLK, None),
            P(WIDE_BLK, None, None, None),
            P(WIDE_BLK, None, None),
            P(WIDE_BLK, None),
        ),
        out_specs=(P(WIDE_BLK, None), P(WIDE_BLK, None)),
        check_vma=False,
    )
```

profile of v0, /device:TPU:1, one launch (start us, length us, event | category | flops | bytes accessed | tf_op | source)
XLA Modules:
  0.0 553.6 jit_solution(8741448501272745176)
XLA Ops:
  7.8 11.9 %all-to-all-start = ((bf16[128,64,256]{2,1,0:T(8,128)(2,1)}), bf16[128,64,256]{2,1,0:T(8,128)(2,1)}, u32[]{:S(2)}, u32[]{:S(2)}) async-start(bf16[128,64,256]{2,1,0:T(8,128)(2,1)} %gather_fusion), calls=%async_computation | async-start | bytes 8388608 | tf_op jit(solution)/shard_map/all_to_all | solution.py:114
  39.9 31.9 %collective-permute-done = bf16[256,256]{1,0:T(8,128)(2,1)S(1)} collective-permute-done((bf16[256,256]{1,0:T(8,128)(2,1)S(1)}, bf16[256,256]{1,0:T(8,128)(2,1)S(1)}, u32[]{:S(2)}, u32[]{:S(2)}) %collective-permute-start) | collective-permute-done | bytes 131104 | tf_op jit(solution)/shard_map/ppermute | solution.py:22
  107.5 14.5 %all-to-all-start.1 = ((f32[4,32,2,256]{3,2,1,0:T(2,128)}), f32[4,32,2,256]{3,2,1,0:T(2,128)S(1)}, u32[]{:S(2)}, u32[]{:S(2)}) async-start(f32[4,32,2,256]{3,2,1,0:T(2,128)} %bitcast.162), calls=%async_computation.1 | async-start | bytes 524288 | tf_op jit(solution)/shard_map/all_to_all | solution.py:35
  139.4 7.8 %all-to-all-start.2 = ((f32[32,2,256]{2,1,0:T(2,128)}), f32[32,2,256]{2,1,0:T(2,128)S(1)}, u32[]{:S(2)}, u32[]{:S(2)}) async-start(f32[32,2,256]{2,1,0:T(2,128)} %reduce_sum.72), calls=%async_computation.2 | async-start | bytes 131072 | tf_op jit(solution)/shard_map/all_to_all | solution.py:43
  158.5 7.3 %all-to-all-done.6 = f32[32,2,256]{2,1,0:T(2,128)S(1)} async-done(((f32[32,2,256]{2,1,0:T(2,128)}), f32[32,2,256]{2,1,0:T(2,128)S(1)}, u32[]{:S(2)}, u32[]{:S(2)}) %all-to-all-start.6) | async-done | bytes 65568 | tf_op jit(solution)/shard_map/all_to_all | solution.py:43
  170.4 7.3 %all-to-all-done.3 = f32[32,2,256]{2,1,0:T(2,128)S(1)} async-done(((f32[32,2,256]{2,1,0:T(2,128)}), f32[32,2,256]{2,1,0:T(2,128)S(1)}, u32[]{:S(2)}, u32[]{:S(2)}) %all-to-all-start.3) | async-done | bytes 65568 | tf_op jit(solution)/shard_map/all_to_all | solution.py:56
  177.8 11.0 %all_to_all.90 = f32[32,2,256]{2,1,0:T(2,128)S(1)} all-to-all(f32[32,2,256]{2,1,0:T(2,128)S(1)} %broadcast_in_dim.18), channel_id=1, replica_groups=mesh['wide_0'=4,'wide_1'=2,'blk_0'=4,'blk_1'=4] {'wide_0','wide_1','blk_0'}, dimensions={0} | all-to-all | bytes 131072 | tf_op jit(solution)/shard_map/all_to_all | solution.py:56
  203.6 11.7 %cholesky.130 = f32[128,128]{1,0:T(8,128)S(1)} custom-call(f32[128,128]{1,0:T(8,128)S(1)} %cholesky.194), custom_call_target="Cholesky" | custom-call | tf_op jit(solution)/shard_map/jit(cholesky)/cholesky | solution.py:130
  215.3 9.8 %custom-call.15 = f32[1,128,128]{1,2,0:T(8,128)S(1)} custom-call(f32[1,128,128]{2,1,0:T(8,128)S(1)} %get-tuple-element.61), custom_call_target="InvertDiagBlocksLowerTriangular" | custom-call | tf_op jit(solution)/shard_map/jit(cholesky)/cholesky | solution.py:130
  225.7 11.7 %cholesky.147 = f32[128,128]{1,0:T(8,128)S(1)} custom-call(f32[128,128]{1,0:T(8,128)S(1)} %convolution_subtract_fusion.7), custom_call_target="Cholesky" | custom-call | tf_op jit(solution)/shard_map/jit(cholesky)/cholesky | solution.py:130
  243.6 20.1 %custom-call.16 = f32[2,128,128]{1,2,0:T(8,128)S(1)} custom-call(f32[2,128,128]{2,1,0:T(8,128)S(1)} %get-tuple-element.18), custom_call_target="InvertDiagBlocksLowerTriangular" | custom-call | tf_op jit(solution)/shard_map/jit(_cho_solve)/triangular_solve | solution.py:131
  265.7 12.2 %fusion.91 = (bf16[4096,256]{1,0:T(8,128)(2,1)S(1)}, f32[4096,256]{1,0:T(8,128)}) fusion(f32[4096,256]{1,0:T(8,128)} %param.10, f32[4096,256]{0,1:T(8,128)} %copy-done.2, f32[128,256]{1,0:T(8,128)S(1)} %fusion.68, f32[128,256]{1,0:T(8,128)S(1)} %fusion.67), kind=kOutput, calls=%fused_computation.143 | convolution fusion | flops 3223388160 | bytes 14942208 | tf_op jit(solution)/shard_map/dot_general | solution.py:133
  282.4 7.4 %all-to-all-start.9 = ((bf16[128,64,256]{2,1,0:T(8,128)(2,1)}), bf16[128,64,256]{2,1,0:T(8,128)(2,1)}, u32[]{:S(2)}, u32[]{:S(2)}) async-start(bf16[128,64,256]{2,1,0:T(8,128)(2,1)} %gather_fusion.2), calls=%async_computation.9 | async-start | bytes 8388608 | tf_op jit(solution)/shard_map/all_to_all | solution.py:114
  303.9 38.0 %collective-permute-done.2 = bf16[256,256]{1,0:T(8,128)(2,1)S(1)} collective-permute-done((bf16[256,256]{1,0:T(8,128)(2,1)S(1)}, bf16[256,256]{1,0:T(8,128)(2,1)S(1)}, u32[]{:S(2)}, u32[]{:S(2)}) %collective-permute-start.2) | collective-permute-done | bytes 131104 | tf_op jit(solution)/shard_map/ppermute | solution.py:22
  379.0 9.9 %fusion.95 = f32[256,256]{1,0:T(8,128)S(1)} fusion(f32[4096,256]{1,0:T(8,128)} %copy-done.3, f32[4096,256]{1,0:T(8,128)} %get-tuple-element.65), kind=kOutput, calls=%fused_computation.147 | convolution fusion | flops 3221225472 | bytes 8650752 | tf_op jit(solution)/shard_map/rs,rt->st/dot_general | solution.py:125
  399.6 7.8 %all-to-all-start.11 = ((f32[32,2,256]{2,1,0:T(2,128)}), f32[32,2,256]{2,1,0:T(2,128)S(1)}, u32[]{:S(2)}, u32[]{:S(2)}) async-start(f32[32,2,256]{2,1,0:T(2,128)} %reduce_sum.76), calls=%async_computation.11 | async-start | bytes 131072 | tf_op jit(solution)/shard_map/all_to_all | solution.py:43
  430.6 7.3 %all-to-all-done.12 = f32[32,2,256]{2,1,0:T(2,128)S(1)} async-done(((f32[32,2,256]{2,1,0:T(2,128)}), f32[32,2,256]{2,1,0:T(2,128)S(1)}, u32[]{:S(2)}, u32[]{:S(2)}) %all-to-all-start.12) | async-done | bytes 65568 | tf_op jit(solution)/shard_map/all_to_all | solution.py:56
  437.9 11.0 %all_to_all.91 = f32[32,2,256]{2,1,0:T(2,128)S(1)} all-to-all(f32[32,2,256]{2,1,0:T(2,128)S(1)} %broadcast_in_dim.23), channel_id=1, replica_groups=mesh['wide_0'=4,'wide_1'=2,'blk_0'=4,'blk_1'=4] {'wide_0','wide_1','blk_0'}, dimensions={0} | all-to-all | bytes 131072 | tf_op jit(solution)/shard_map/all_to_all | solution.py:56
  453.1 12.6 %convolution_bitcast_fusion = f32[4096,256]{0,1:T(8,128)} fusion(f32[4096,256]{1,0:T(8,128)} %param.10, f32[128,256]{1,0:T(8,128)S(1)} %fusion.68, f32[128,256]{1,0:T(8,128)S(1)} %fusion.67), kind=kOutput, calls=%fused_computation.11 | convolution fusion | flops 3221291008 | bytes 8650752 | tf_op jit(solution)/shard_map/dot_general | solution.py:132
  471.4 11.7 %cholesky.164 = f32[128,128]{1,0:T(8,128)S(1)} custom-call(f32[128,128]{1,0:T(8,128)S(1)} %cholesky.197), custom_call_target="Cholesky" | custom-call | tf_op jit(solution)/shard_map/jit(cholesky)/cholesky | solution.py:130
  483.2 9.8 %custom-call.17 = f32[1,128,128]{1,2,0:T(8,128)S(1)} custom-call(f32[1,128,128]{2,1,0:T(8,128)S(1)} %get-tuple-element.57), custom_call_target="InvertDiagBlocksLowerTriangular" | custom-call | tf_op jit(solution)/shard_map/jit(cholesky)/cholesky | solution.py:130
  493.5 11.7 %cholesky.181 = f32[128,128]{1,0:T(8,128)S(1)} custom-call(f32[128,128]{1,0:T(8,128)S(1)} %convolution_subtract_fusion.6), custom_call_target="Cholesky" | custom-call | tf_op jit(solution)/shard_map/jit(cholesky)/cholesky | solution.py:130
  511.5 19.8 %custom-call.18 = f32[2,128,128]{1,2,0:T(8,128)S(1)} custom-call(f32[2,128,128]{2,1,0:T(8,128)S(1)} %get-tuple-element.19), custom_call_target="InvertDiagBlocksLowerTriangular" | custom-call | tf_op jit(solution)/shard_map/jit(_cho_solve)/triangular_solve | solution.py:131
  533.4 9.0 %convolution_subtract_fusion = f32[4096,256]{1,0:T(8,128)} fusion(f32[4096,256]{1,0:T(8,128)} %get-tuple-element.65, f32[4096,256]{1,0:T(8,128)} %copy-done.3, f32[128,256]{1,0:T(8,128)S(1)} %fusion.71, f32[128,256]{1,0:T(8,128)S(1)} %fusion.70), kind=kOutput, calls=%fused_computation.8 | convolution fusion | flops 3222339584 | bytes 12845056 | tf_op jit(solution)/shard_map/dot_general | solution.py:133
  (177 shorter events, 244.0 us)
Async XLA Ops:
  0.6 84.4 %copy-start = (bf16[32,4,64,64]{3,2,1,0:T(8,128)(2,1)S(1)}, bf16[32,4,64,64]{3,2,1,0:T(8,128)(2,1)}, u32[]{:S(2)}) copy-start(bf16[32,4,64,64]{3,2,1,0:T(8,128)(2,1)} %param.14) | copy-start | bytes 3145732
  7.8 72.1 %all-to-all-start = ((bf16[128,64,256]{2,1,0:T(8,128)(2,1)}), bf16[128,64,256]{2,1,0:T(8,128)(2,1)}, u32[]{:S(2)}, u32[]{:S(2)}) async-start(bf16[128,64,256]{2,1,0:T(8,128)(2,1)} %gather_fusion), calls=%async_computation | async-start | bytes 8388608 | tf_op jit(solution)/shard_map/all_to_all | solution.py:114
  20.8 51.1 %collective-permute-start = (bf16[256,256]{1,0:T(8,128)(2,1)S(1)}, bf16[256,256]{1,0:T(8,128)(2,1)S(1)}, u32[]{:S(2)}, u32[]{:S(2)}) collective-permute-start(bf16[256,256]{1,0:T(8,128)(2,1)S(1)} %get-tuple-element.52), channel_id=1, source_target_pairs={{0,1},{1,2},{2,3},{3,4},{4,5},{5,6},{6,7},{7,8},{8,9},{9,10},{10,1... | collective-permute-start | bytes 393224 | tf_op jit(solution)/shard_map/ppermute | solution.py:22
  22.2 53.8 %collective-permute-start.1 = (bf16[256,256]{1,0:T(8,128)(2,1)S(1)}, bf16[256,256]{1,0:T(8,128)(2,1)S(1)}, u32[]{:S(2)}, u32[]{:S(2)}) collective-permute-start(bf16[256,256]{1,0:T(8,128)(2,1)S(1)} %get-tuple-element.53), channel_id=1, source_target_pairs={{1,0},{2,1},{3,2},{4,3},{5,4},{6,5},{7,6},{8,7},{9,8},{10,9},{11,1... | collective-permute-start | bytes 393224 | tf_op jit(solution)/shard_map/ppermute | solution.py:23
  39.9 36.1 %copy-start.6 = (bf16[4096,256]{1,0:T(8,128)(2,1)S(1)}, bf16[4096,256]{1,0:T(8,128)(2,1)}, u32[]{:S(2)}) copy-start(bf16[4096,256]{1,0:T(8,128)(2,1)} %copy-done.5) | copy-start | bytes 6291460
  107.5 22.5 %all-to-all-start.1 = ((f32[4,32,2,256]{3,2,1,0:T(2,128)}), f32[4,32,2,256]{3,2,1,0:T(2,128)S(1)}, u32[]{:S(2)}, u32[]{:S(2)}) async-start(f32[4,32,2,256]{3,2,1,0:T(2,128)} %bitcast.162), calls=%async_computation.1 | async-start | bytes 524288 | tf_op jit(solution)/shard_map/all_to_all | solution.py:35
  130.0 9.4 %all-to-all-start.5 = ((f32[4,32,2,256]{3,2,1,0:T(2,128)}), f32[4,32,2,256]{3,2,1,0:T(2,128)S(1)}, u32[]{:S(2)}, u32[]{:S(2)}) async-start(f32[4,32,2,256]{3,2,1,0:T(2,128)} %bitcast.161), calls=%async_computation.5 | async-start | bytes 524288 | tf_op jit(solution)/shard_map/all_to_all | solution.py:35
  139.4 15.1 %all-to-all-start.2 = ((f32[32,2,256]{2,1,0:T(2,128)}), f32[32,2,256]{2,1,0:T(2,128)S(1)}, u32[]{:S(2)}, u32[]{:S(2)}) async-start(f32[32,2,256]{2,1,0:T(2,128)} %reduce_sum.72), calls=%async_computation.2 | async-start | bytes 131072 | tf_op jit(solution)/shard_map/all_to_all | solution.py:43
  154.5 11.3 %all-to-all-start.6 = ((f32[32,2,256]{2,1,0:T(2,128)}), f32[32,2,256]{2,1,0:T(2,128)S(1)}, u32[]{:S(2)}, u32[]{:S(2)}) async-start(f32[32,2,256]{2,1,0:T(2,128)} %reduce_sum.74), calls=%async_computation.6 | async-start | bytes 131072 | tf_op jit(solution)/shard_map/all_to_all | solution.py:43
  166.5 11.3 %all-to-all-start.3 = ((f32[32,2,256]{2,1,0:T(2,128)}), f32[32,2,256]{2,1,0:T(2,128)S(1)}, u32[]{:S(2)}, u32[]{:S(2)}) async-start(f32[32,2,256]{2,1,0:T(2,128)} %broadcast_in_dim.16), calls=%async_computation.3 | async-start | bytes 131072 | tf_op jit(solution)/shard_map/all_to_all | solution.py:56
  189.5 9.5 %all-to-all-start.4 = ((f32[4,32,2,256]{3,2,1,0:T(2,128)}), f32[4,32,2,256]{3,2,1,0:T(2,128)S(1)}, u32[]{:S(2)}, u32[]{:S(2)}) async-start(f32[4,32,2,256]{3,2,1,0:T(2,128)} %broadcast_in_dim.17), calls=%async_computation.4 | async-start | bytes 524288 | tf_op jit(solution)/shard_map/all_to_all | solution.py:56
  199.7 63.9 %all-to-all-start.8 = ((f32[4,32,2,256]{3,2,1,0:T(2,128)}), f32[4,32,2,256]{3,2,1,0:T(2,128)S(1)}, u32[]{:S(2)}, u32[]{:S(2)}) async-start(f32[4,32,2,256]{3,2,1,0:T(2,128)} %broadcast_in_dim.20), calls=%async_computation.8 | async-start | bytes 524288 | tf_op jit(solution)/shard_map/all_to_all | solution.py:56
  265.7 13.5 %copy-start.10 = (bf16[4096,64]{0,1:T(8,128)(2,1)S(1)}, bf16[4096,64]{0,1:T(8,128)(2,1)}, u32[]{:S(2)}) copy-start(bf16[4096,64]{0,1:T(8,128)(2,1)} %param.12) | copy-start | bytes 1572868
  282.4 67.3 %all-to-all-start.9 = ((bf16[128,64,256]{2,1,0:T(8,128)(2,1)}), bf16[128,64,256]{2,1,0:T(8,128)(2,1)}, u32[]{:S(2)}, u32[]{:S(2)}) async-start(bf16[128,64,256]{2,1,0:T(8,128)(2,1)} %gather_fusion.2), calls=%async_computation.9 | async-start | bytes 8388608 | tf_op jit(solution)/shard_map/all_to_all | solution.py:114
  290.8 51.1 %collective-permute-start.2 = (bf16[256,256]{1,0:T(8,128)(2,1)S(1)}, bf16[256,256]{1,0:T(8,128)(2,1)S(1)}, u32[]{:S(2)}, u32[]{:S(2)}) collective-permute-start(bf16[256,256]{1,0:T(8,128)(2,1)S(1)} %get-tuple-element.50), channel_id=1, source_target_pairs={{0,1},{1,2},{2,3},{3,4},{4,5},{5,6},{6,7},{7,8},{8,9},{9,10},{10,1... | collective-permute-start | bytes 393224 | tf_op jit(solution)/shard_map/ppermute | solution.py:22
  300.3 45.5 %collective-permute-start.3 = (bf16[256,256]{1,0:T(8,128)(2,1)S(1)}, bf16[256,256]{1,0:T(8,128)(2,1)S(1)}, u32[]{:S(2)}, u32[]{:S(2)}) collective-permute-start(bf16[256,256]{1,0:T(8,128)(2,1)S(1)} %get-tuple-element.51), channel_id=1, source_target_pairs={{1,0},{2,1},{3,2},{4,3},{5,4},{6,5},{7,6},{8,7},{9,8},{10,9},{11,1... | collective-permute-start | bytes 393224 | tf_op jit(solution)/shard_map/ppermute | solution.py:23
  375.4 14.4 %all-to-all-start.10 = ((f32[4,32,2,256]{3,2,1,0:T(2,128)}), f32[4,32,2,256]{3,2,1,0:T(2,128)S(1)}, u32[]{:S(2)}, u32[]{:S(2)}) async-start(f32[4,32,2,256]{3,2,1,0:T(2,128)} %bitcast.160), calls=%async_computation.10 | async-start | bytes 524288 | tf_op jit(solution)/shard_map/all_to_all | solution.py:35
  389.8 9.7 %all-to-all-start.14 = ((f32[4,32,2,256]{3,2,1,0:T(2,128)}), f32[4,32,2,256]{3,2,1,0:T(2,128)S(1)}, u32[]{:S(2)}, u32[]{:S(2)}) async-start(f32[4,32,2,256]{3,2,1,0:T(2,128)} %bitcast.159), calls=%async_computation.14 | async-start | bytes 524288 | tf_op jit(solution)/shard_map/all_to_all | solution.py:35
  399.6 15.1 %all-to-all-start.11 = ((f32[32,2,256]{2,1,0:T(2,128)}), f32[32,2,256]{2,1,0:T(2,128)S(1)}, u32[]{:S(2)}, u32[]{:S(2)}) async-start(f32[32,2,256]{2,1,0:T(2,128)} %reduce_sum.76), calls=%async_computation.11 | async-start | bytes 131072 | tf_op jit(solution)/shard_map/all_to_all | solution.py:43
  414.7 11.3 %all-to-all-start.15 = ((f32[32,2,256]{2,1,0:T(2,128)}), f32[32,2,256]{2,1,0:T(2,128)S(1)}, u32[]{:S(2)}, u32[]{:S(2)}) async-start(f32[32,2,256]{2,1,0:T(2,128)} %reduce_sum.78), calls=%async_computation.15 | async-start | bytes 131072 | tf_op jit(solution)/shard_map/all_to_all | solution.py:43
  426.6 11.3 %all-to-all-start.12 = ((f32[32,2,256]{2,1,0:T(2,128)}), f32[32,2,256]{2,1,0:T(2,128)S(1)}, u32[]{:S(2)}, u32[]{:S(2)}) async-start(f32[32,2,256]{2,1,0:T(2,128)} %broadcast_in_dim.21), calls=%async_computation.12 | async-start | bytes 131072 | tf_op jit(solution)/shard_map/all_to_all | solution.py:56
  449.6 16.0 %all-to-all-start.13 = ((f32[4,32,2,256]{3,2,1,0:T(2,128)}), f32[4,32,2,256]{3,2,1,0:T(2,128)S(1)}, u32[]{:S(2)}, u32[]{:S(2)}) async-start(f32[4,32,2,256]{3,2,1,0:T(2,128)} %broadcast_in_dim.22), calls=%async_computation.13 | async-start | bytes 524288 | tf_op jit(solution)/shard_map/all_to_all | solution.py:56
  466.4 65.0 %all-to-all-start.17 = ((f32[4,32,2,256]{3,2,1,0:T(2,128)}), f32[4,32,2,256]{3,2,1,0:T(2,128)S(1)}, u32[]{:S(2)}, u32[]{:S(2)}) async-start(f32[4,32,2,256]{3,2,1,0:T(2,128)} %broadcast_in_dim.24), calls=%async_computation.17 | async-start | bytes 524288 | tf_op jit(solution)/shard_map/all_to_all | solution.py:56
  533.4 9.1 %copy-start.1 = (f32[4096,256]{1,0:T(8,128)S(1)}, f32[4096,256]{1,0:T(8,128)}, u32[]{:S(2)}) copy-start(f32[4096,256]{1,0:T(8,128)} %get-tuple-element.65) | copy-start | bytes 12582916
  (12 other events, 47.8 us)
where the time goes:
time: 553 us; the launch traced here: 554 us
  waiting for transfers between devices  128 us (23%)
  other arithmetic  124 us (22%)
  matrix products  115 us (21%)
  starting transfers between devices  102 us (18%)
  local copies, waits for them, and re-layouts  58.4 us (11%)
  blocking collectives  21.9 us (4%)
    ppermute x2, waiting for transfers between devices, with_halo(): before = lax.ppermute(last, axis, up)  69.9 us
    another operation x13, other arithmetic, shards(): factor = jnp.linalg.cholesky(gram)  68.6 us
    another operation x5, other arithmetic, shards(): alpha = jax.scipy.linalg.cho_solve((factor, True), proj)  40 us
    dot_general x8, matrix products, near_apply(): jnp.dot(near_rows[j * NEAR:(j + 1) * NEAR], ext[j * NEAR:j * NEAR + NEAR...  32 us
    all_to_all x4, waiting for transfers between devices, sum_by_axis(): lax.all_to_all(nearer, far, split_axis=0, concat_axis=0, tiled=True)  27.7 us
    all_to_all x4, starting transfers between devices, summed_on_arrival(): lax.all_to_all(parts, axis, split_axis=0, concat_axis=0, tiled=True)  26.3 us
    all_to_all x4, starting transfers between devices, sum_by_axis(): lax.all_to_all(nearer, far, split_axis=0, concat_axis=0, tiled=True)  23.5 us
    all_to_all x6, starting transfers between devices, copy_for_each(): lax.all_to_all(jnp.broadcast_to(value[None], (count, *value.shape)), axis...  22.7 us
  transfers between devices with their start and end apart: 20, of which 11 were waited for; matrix products, arithmetic and copies ran while one was open for 35% of the time, Pallas kernels for 0%

commit v1 on v0

v1 whole, which is shorter than its diff:
```python
import jax
import jax.numpy as jnp
from jax import lax
from jax.experimental import pallas as pl
from jax.experimental.pallas import tpu as pltpu
from jax.sharding import Mesh
from jax.sharding import PartitionSpec as P

NEAR = 1024
HALO = 256
LEAF = 128
RANK = 64
WIDTH = 256
TILE = 512
BLK = ("blk_0", "blk_1")
WIDE_BLK = ("wide_0", "wide_1", "blk_0", "blk_1")
F32 = jnp.float32
BF16 = jnp.bfloat16
HIGHEST = lax.Precision.HIGHEST


def params(mib):
    return pltpu.CompilerParams(
        dimension_semantics=("arbitrary",), vmem_limit_bytes=mib * 1024 * 1024
    )


def whole(*shape):
    return pl.BlockSpec(shape, lambda t: (0,) * len(shape))


def tiled(*shape):
    return pl.BlockSpec(shape, lambda t: (t,) + (0,) * (len(shape) - 1))


def smem():
    return pl.BlockSpec(memory_space=pltpu.SMEM)


def hbm():
    return pl.BlockSpec(memory_space=pltpu.HBM)


def dot(a, b):
    return jnp.dot(a, b, preferred_element_type=F32)


def dot_t(a, b):
    return lax.dot_general(a, b, (((0,), (0,)), ((), ())), preferred_element_type=F32)


def halves(x):
    hi = x.astype(BF16)
    return hi, (x - hi.astype(F32)).astype(BF16)


def dot3(x, hi, lo):
    xh, xl = halves(x)
    return dot(xh, hi) + (dot(xl, hi) + dot(xh, lo))


def send_rows(packed, ids, out, sem, count):
    def one(d, carry):
        pltpu.make_async_copy(packed.at[ids[d]], out.at[d], sem).start()
        return carry

    lax.fori_loop(0, count, one, 0, unroll=8)
    pltpu.make_async_copy(out, out, sem).wait()


def front_kernel(ids, r, s, out, packed, sem):
    t = pl.program_id(0)
    vb = r[...].astype(BF16)
    per = TILE // LEAF
    for i in range(per):
        rows = slice(i * LEAF, (i + 1) * LEAF)
        packed[t * per + i] = dot_t(s[rows], vb[rows]).astype(BF16)

    @pl.when(t == pl.num_programs(0) - 1)
    def _():
        send_rows(packed, ids, out, sem, out.shape[0])


def front(ids, r, s):
    rows = r.shape[0]
    count = ids.shape[0]
    return pl.pallas_call(
        front_kernel,
        grid=(rows // TILE,),
        in_specs=[smem(), tiled(TILE, WIDTH), tiled(TILE, RANK)],
        out_specs=hbm(),
        out_shape=jax.ShapeDtypeStruct((count, RANK, WIDTH), BF16),
        scratch_shapes=[
            pltpu.VMEM((rows // LEAF, RANK, WIDTH), BF16),
            pltpu.SemaphoreType.DMA(()),
        ],
        compiler_params=params(16),
        name="front",
    )(ids, r, s)


def near0_kernel(r, lo, hi, near, s, base, err, ext):
    t = pl.program_id(0)
    rows = r.shape[0]

    @pl.when(t == 0)
    def _():
        ext[:HALO] = lo[...].astype(BF16)
        ext[HALO : HALO + rows] = r[...].astype(BF16)
        ext[HALO + rows :] = hi[...].astype(BF16)

    first = pl.multiple_of((t // (NEAR // TILE)) * NEAR, NEAR)
    own = r[pl.ds(pl.multiple_of(t * TILE, TILE), TILE)]
    base[...] = own + dot(near[...], ext[pl.ds(first, NEAR + 2 * HALO)])
    rh, rl = halves(own)
    for i in range(TILE // LEAF):
        cut = slice(i * LEAF, (i + 1) * LEAF)
        high = dot_t(s[cut], rh[cut])
        low = dot_t(s[cut], rl[cut])
        err[i] = (high.astype(BF16).astype(F32) - high) - low


def near0(r, lo, hi, near, s):
    rows = r.shape[0]
    per = TILE // LEAF
    return pl.pallas_call(
        near0_kernel,
        grid=(rows // TILE,),
        in_specs=[
            whole(rows, WIDTH),
            whole(HALO, WIDTH),
            whole(HALO, WIDTH),
            tiled(TILE, NEAR + 2 * HALO),
            tiled(TILE, RANK),
        ],
        out_specs=[tiled(TILE, WIDTH), tiled(per, RANK, WIDTH)],
        out_shape=[
            jax.ShapeDtypeStruct((rows, WIDTH), F32),
            jax.ShapeDtypeStruct((rows // LEAF, RANK, WIDTH), F32),
        ],
        scratch_shapes=[pltpu.VMEM((rows + 2 * HALO, WIDTH), BF16)],
        compiler_params=params(32),
        cost_estimate=pl.CostEstimate(flops=4_000_000_000, bytes_accessed=24_000_000, transcendentals=0),
        name="near0",
    )(r, lo, hi, near, s)


def gram_step(t, image, r, acc):
    ih, il = halves(image)
    rh, rl = halves(r)

    @pl.when(t == 0)
    def _():
        acc[...] = jnp.zeros(acc.shape, F32)

    turned = ih.T
    left = jnp.concatenate([turned, turned, il.T], axis=1)
    gram = jnp.concatenate([ih, il, ih], axis=0)
    proj = jnp.concatenate([rh, rl, rh], axis=0)
    acc[...] += dot(left, jnp.concatenate([gram, proj], axis=1))
    return ih, il


def gram_end(acc, out):
    for i in range(WIDTH // 8):
        cut = slice(8 * i, 8 * i + 8)
        for h in range(2):
            out[2 * i + h] = acc[cut, 128 * h : 128 * h + 128]
            out[64 + 2 * i + h] = acc[cut, WIDTH + 128 * h : WIDTH + 128 * h + 128]


def slots_of(readers, incoming, leaf):
    return jnp.concatenate([incoming[readers[leaf * 4 + f]] for f in range(4)], axis=0)


def far0_kernel(ids, readers, incoming, coup, tb, s, base, r, err, image, trans, gp, out, packed, direct, acc, sem):
    t = pl.program_id(0)
    per = TILE // LEAF
    tiles = []
    for i in range(per):
        cut = slice(i * LEAF, (i + 1) * LEAF)
        tr = dot(coup[i * RANK : (i + 1) * RANK], slots_of(readers, incoming, t * per + i))
        trans[i * RANK : (i + 1) * RANK] = tr
        tiles.append(base[cut] + dot(tb[cut], tr.astype(BF16)))
    value = jnp.concatenate(tiles, axis=0)
    image[...] = value
    ih, il = gram_step(t, value, r[...], acc)
    for i in range(per):
        cut = slice(i * LEAF, (i + 1) * LEAF)
        direct[t * per + i] = dot_t(s[cut], ih[cut]) + dot_t(s[cut], il[cut])

    @pl.when(t == pl.num_programs(0) - 1)
    def _():
        gram_end(acc, gp)
        gram, total = acc[:, :WIDTH], acc[:, WIDTH:]
        eye = lax.broadcasted_iota(jnp.int32, gram.shape, 0) == lax.broadcasted_iota(jnp.int32, gram.shape, 1)
        g = jnp.sum(jnp.where(eye, gram, 0.0), axis=0, keepdims=True)
        p = jnp.sum(jnp.where(eye, total, 0.0), axis=0, keepdims=True)
        fits = (4.0 * p > g) & (4.0 * g > p)
        guess = jnp.where(fits, g / jnp.where(fits, p, 1.0), 0.0)
        for leaf in range(packed.shape[0]):
            packed[leaf] = (direct[leaf] + err[leaf] * guess).astype(BF16)
        send_rows(packed, ids, out, sem, out.shape[0])


def far0(ids, readers, incoming, coup, tb, s, base, r, err):
    rows = r.shape[0]
    leaves = rows // LEAF
    count = ids.shape[0]
    per = TILE // LEAF
    return pl.pallas_call(
        far0_kernel,
        grid=(rows // TILE,),
        in_specs=[
            smem(),
            smem(),
            whole(count, RANK, WIDTH),
            tiled(per * RANK, 4 * RANK),
            tiled(TILE, RANK),
            tiled(TILE, RANK),
            tiled(TILE, WIDTH),
            tiled(TILE, WIDTH),
            whole(leaves, RANK, WIDTH),
        ],
        out_specs=[tiled(TILE, WIDTH), tiled(per * RANK, WIDTH), whole(128, 8, 128), hbm()],
        out_shape=[
            jax.ShapeDtypeStruct((rows, WIDTH), F32),
            jax.ShapeDtypeStruct((leaves * RANK, WIDTH), F32),
            jax.ShapeDtypeStruct((128, 8, 128), F32),
            jax.ShapeDtypeStruct((count, RANK, WIDTH), BF16),
        ],
        scratch_shapes=[
            pltpu.VMEM((leaves, RANK, WIDTH), BF16),
            pltpu.VMEM((leaves, RANK, WIDTH), F32),
            pltpu.VMEM((WIDTH, 2 * WIDTH), F32),
            pltpu.SemaphoreType.DMA(()),
        ],
        compiler_params=params(40),
        name="far0",
    )(ids, readers, incoming, coup, tb, s, base, r, err)


def sum_kernel(parts, out):
    total = jnp.sum(parts[...], axis=0)
    out[...] = jnp.broadcast_to(total[None], out.shape)


def summed(parts):
    return pl.pallas_call(
        sum_kernel,
        out_shape=jax.ShapeDtypeStruct(parts.shape, F32),
        compiler_params=pltpu.CompilerParams(vmem_limit_bytes=8 * 1024 * 1024),
        name="summed",
    )(parts)


def lane(x, c):
    return jnp.broadcast_to(x[:, c : c + 1], (8, 128))


def sub(x, k):
    return jnp.broadcast_to(x[k : k + 1, :], (8, 128))


def inverse(rows):
    lanes = lax.broadcasted_iota(jnp.int32, (8, 128), 1)
    subs = lax.broadcasted_iota(jnp.int32, (8, 128), 0)
    rows = list(rows)
    count = len(rows)
    for p in range(count):
        pivot = rows[p]
        cols = [lane(pivot, 8 * p + j) for j in range(8)]
        for k in range(8):
            inv = 1.0 / sub(cols[k], k)
            ck = cols[k]
            here = subs == k
            scaled = sub(pivot, k) * inv
            pivot = jnp.where(here, scaled, pivot - ck * scaled)
            for j in range(8):
                if j != k:
                    cj = sub(cols[j], k) * inv
                    cols[j] = jnp.where(here, cj, cols[j] - ck * cj)
            cols[k] = jnp.where(here, inv, -ck * inv)
            pivot = jnp.where(lanes == 8 * p + k, cols[k], pivot)
        spread = [sub(pivot, j) for j in range(8)]
        panel = (lanes >= 8 * p) & (lanes < 8 * p + 8)
        for i in range(count):
            if i != p:
                value = jnp.where(panel, 0.0, rows[i])
                for j in range(8):
                    value = value - lane(rows[i], 8 * p + j) * spread[j]
                rows[i] = value
        rows[p] = pivot
    return rows


def exact(a, b):
    return jnp.dot(a, b, preferred_element_type=F32, precision=HIGHEST)


def solve_kernel(gp, alpha, high, low):
    def block(first, i0, i1, h):
        return jnp.concatenate([gp[first + 2 * i + h] for i in range(i0, i1)], axis=0)

    x11 = jnp.concatenate(inverse([gp[2 * i] for i in range(16)]), axis=0)
    a12 = block(0, 0, 16, 1)
    a21 = block(0, 16, 32, 0)
    w = exact(x11, a12)
    b1 = jnp.concatenate([block(64, 0, 16, 0), block(64, 0, 16, 1)], axis=1)
    b2 = jnp.concatenate([block(64, 16, 32, 0), block(64, 16, 32, 1)], axis=1)
    schur = block(0, 16, 32, 1) - exact(a21, w)
    y1 = exact(x11, b1)
    z = b2 - exact(a21, y1)
    x22 = jnp.concatenate(inverse([schur[8 * i : 8 * i + 8] for i in range(16)]), axis=0)
    lower = exact(x22, z)
    upper = y1 - exact(w, lower)
    value = jnp.concatenate([upper, lower], axis=0)
    alpha[...] = value
    hi, lo = halves(value)
    high[...] = hi
    low[...] = lo


def solve(gp):
    return pl.pallas_call(
        solve_kernel,
        out_shape=[
            jax.ShapeDtypeStruct((WIDTH, WIDTH), F32),
            jax.ShapeDtypeStruct((WIDTH, WIDTH), BF16),
            jax.ShapeDtypeStruct((WIDTH, WIDTH), BF16),
        ],
        compiler_params=pltpu.CompilerParams(vmem_limit_bytes=16 * 1024 * 1024),
        cost_estimate=pl.CostEstimate(flops=12_000_000_000, bytes_accessed=1_000_000, transcendentals=0),
        name="solve",
    )(gp)


def near1_kernel(r, lo, hi, image, ilo, ihi, ah, al, near, resid, base, sol, ext, full):
    t = pl.program_id(0)
    rows = r.shape[0]
    high, low = ah[...], al[...]

    @pl.when(t == 0)
    def _():
        ext[:HALO] = (lo[...] - dot3(ilo[...], high, low)).astype(BF16)
        for c in range(rows // TILE):
            cut = slice(c * TILE, (c + 1) * TILE)
            value = r[cut] - dot3(image[cut], high, low)
            full[cut] = value
            ext[HALO + c * TILE : HALO + (c + 1) * TILE] = value.astype(BF16)
        ext[HALO + rows :] = (hi[...] - dot3(ihi[...], high, low)).astype(BF16)

    first = pl.multiple_of((t // (NEAR // TILE)) * NEAR, NEAR)
    here = pl.ds(pl.multiple_of(t * TILE, TILE), TILE)
    own = full[here]
    resid[...] = own
    base[...] = own + dot(near[...], ext[pl.ds(first, NEAR + 2 * HALO)])
    sol[...] = dot3(r[here], high, low)


def near1(r, lo, hi, image, ilo, ihi, ah, al, near):
    rows = r.shape[0]
    return pl.pallas_call(
        near1_kernel,
        grid=(rows // TILE,),
        in_specs=[
            whole(rows, WIDTH),
            whole(HALO, WIDTH),
            whole(HALO, WIDTH),
            whole(rows, WIDTH),
            whole(HALO, WIDTH),
            whole(HALO, WIDTH),
            whole(WIDTH, WIDTH),
            whole(WIDTH, WIDTH),
            tiled(TILE, NEAR + 2 * HALO),
        ],
        out_specs=[tiled(TILE, WIDTH)] * 3,
        out_shape=[jax.ShapeDtypeStruct((rows, WIDTH), F32)] * 3,
        scratch_shapes=[
            pltpu.VMEM((rows + 2 * HALO, WIDTH), BF16),
            pltpu.VMEM((rows, WIDTH), F32),
        ],
        compiler_params=params(48),
        cost_estimate=pl.CostEstimate(flops=8_000_000_000, bytes_accessed=36_000_000, transcendentals=0),
        name="near1",
    )(r, lo, hi, image, ilo, ihi, ah, al, near)


def far1_kernel(readers, incoming, coup, tb, base, r, trans, ah, al, image, gp, acc):
    t = pl.program_id(0)
    per = TILE // LEAF
    moved = jnp.concatenate(
        [
            dot(coup[i * RANK : (i + 1) * RANK], slots_of(readers, incoming, t * per + i))
            for i in range(per)
        ],
        axis=0,
    )
    tr = (trans[...] - dot3(moved, ah[...], al[...])).astype(BF16)
    tiles = []
    for i in range(per):
        cut = slice(i * LEAF, (i + 1) * LEAF)
        tiles.append(base[cut] + dot(tb[cut], tr[i * RANK : (i + 1) * RANK]))
    value = jnp.concatenate(tiles, axis=0)
    image[...] = value
    gram_step(t, value, r[...], acc)

    @pl.when(t == pl.num_programs(0) - 1)
    def _():
        gram_end(acc, gp)


def far1(readers, incoming, coup, tb, base, r, trans, ah, al):
    rows = r.shape[0]
    count = incoming.shape[0]
    per = TILE // LEAF
    return pl.pallas_call(
        far1_kernel,
        grid=(rows // TILE,),
        in_specs=[
            smem(),
            whole(count, RANK, WIDTH),
            tiled(per * RANK, 4 * RANK),
            tiled(TILE, RANK),
            tiled(TILE, WIDTH),
            tiled(TILE, WIDTH),
            tiled(per * RANK, WIDTH),
            whole(WIDTH, WIDTH),
            whole(WIDTH, WIDTH),
        ],
        out_specs=[tiled(TILE, WIDTH), whole(128, 8, 128)],
        out_shape=[
            jax.ShapeDtypeStruct((rows, WIDTH), F32),
            jax.ShapeDtypeStruct((128, 8, 128), F32),
        ],
        scratch_shapes=[
            pltpu.VMEM((WIDTH, 2 * WIDTH), F32),
        ],
        compiler_params=params(32),
        name="far1",
    )(readers, incoming, coup, tb, base, r, trans, ah, al)


def finish_kernel(sol, r, image, ah, al, solution, residual):
    high, low = ah[...], al[...]
    solution[...] = sol[...] + dot3(r[...], high, low)
    residual[...] = r[...] - dot3(image[...], high, low)


def finish(sol, r, image, ah, al):
    rows = r.shape[0]
    return pl.pallas_call(
        finish_kernel,
        grid=(rows // TILE,),
        in_specs=[tiled(TILE, WIDTH)] * 3 + [whole(WIDTH, WIDTH)] * 2,
        out_specs=[tiled(TILE, WIDTH)] * 2,
        out_shape=[jax.ShapeDtypeStruct((rows, WIDTH), F32)] * 2,
        compiler_params=params(16),
        name="finish",
    )(sol, r, image, ah, al)


def exchange(value):
    return lax.all_to_all(value, WIDE_BLK, split_axis=0, concat_axis=0, tiled=True)


def sides(value):
    count = lax.axis_size(BLK)
    up = [(i, (i + 1) % count) for i in range(count)]
    down = [(j, i) for i, j in up]
    before = lax.ppermute(value[-HALO:], BLK, up)
    after = lax.ppermute(value[:HALO], BLK, down)
    return before, after


def shards(rhs, near_blocks, source_basis, target_basis, far_coupling, send_ids, far_list):
    leaves = rhs.shape[0] // LEAF
    ids = send_ids.reshape(-1)
    readers = far_list.reshape(-1)
    coup = far_coupling.transpose(0, 2, 1, 3).reshape(leaves * RANK, 4 * RANK)
    lo, hi = sides(rhs)
    incoming = exchange(front(ids, rhs, source_basis))
    base0, err = near0(rhs, lo, hi, near_blocks, source_basis)
    image0, trans0, gp0, outgoing = far0(
        ids, readers, incoming, coup, target_basis, source_basis, base0, rhs, err
    )
    parts = exchange(gp0)
    ilo, ihi = sides(image0)
    total = summed(parts)
    total, outgoing = lax.optimization_barrier((total, outgoing))
    whole0 = exchange(total)
    incoming1 = exchange(outgoing)
    _, ah, al = solve(whole0)
    r1, base1, sol = near1(rhs, lo, hi, image0, ilo, ihi, ah, al, near_blocks)
    image1, gp1 = far1(readers, incoming1, coup, target_basis, base1, r1, trans0, ah, al)
    whole1 = exchange(summed(exchange(gp1)))
    _, bh, bl = solve(whole1)
    return tuple(finish(sol, r1, image1, bh, bl))


def solution(mesh):
    split = Mesh(mesh.devices.reshape(4, 2, 4, 4), ("wide_0", "wide_1", "blk_0", "blk_1"))
    return jax.shard_map(
        shards,
        mesh=split,
        in_specs=(
            P(WIDE_BLK, None),
            P(WIDE_BLK, None),
            P(WIDE_BLK, None),
            P(WIDE_BLK, None),
            P(WIDE_BLK, None, None, None),
            P(WIDE_BLK, None, None),
            P(WIDE_BLK, None),
        ),
        out_specs=(P(WIDE_BLK, None), P(WIDE_BLK, None)),
        check_vma=False,
    )
```

time: 553 us -> 311 us (0.56)
  other arithmetic: 124 us -> 0 us
  matrix products: 115 us -> 0 us
  Pallas kernels: 0 us -> 90.3 us
  starting transfers between devices: 102 us -> 27 us
  blocking collectives: 21.9 us -> 76.3 us
  waiting for transfers between devices: 128 us -> 78.6 us
  local copies, waits for them, and re-layouts: 58.4 us -> 36.6 us
    dot_general x20 -> x0, matrix products: 111 us -> none  [the longest x8 32 us: near_apply(): jnp.dot(near_rows[j * NEAR:(j + 1) * NEAR], ext[j * NEAR:j * NEAR + NEAR...]
    another operation x18 -> x0, other arithmetic: 109 us -> none  [the longest x13 68.6 us: shards(): factor = jnp.linalg.cholesky(gram)]
    pallas_call x0 -> x10, Pallas kernels: none -> 90.3 us  [the longest x2 19.6 us: solve(): pl.pallas_call(solve_kernel, out_shape=[jax.ShapeDtypeStruct((WIDTH, WIDT...]
    all_to_all x16 -> x2, starting transfers between devices: 91.8 us -> 17.3 us  [exchange(): lax.all_to_all(value, WIDE_BLK, split_axis=0, concat_axis=0, tiled=True)]
    all_to_all x16 -> x2, waiting for transfers between devices: 57.9 us -> 0.01 us  [exchange(): lax.all_to_all(value, WIDE_BLK, split_axis=0, concat_axis=0, tiled=True)]
    all_to_all x2 -> x4, blocking collectives: 21.9 us -> 76.3 us  [exchange(): lax.all_to_all(value, WIDE_BLK, split_axis=0, concat_axis=0, tiled=True)]
    gather x4 -> x0, local copies, waits for them, and re-layouts: 15.8 us -> none  [the longest x2 10.1 us: shards(): picked = incoming[readers].reshape(leaves, fanout, rank, width)]
    another operation x33 -> x0, local copies, waits for them, and re-layouts: 12.4 us -> none  [the longest x15 7.78 us: shards(): alpha = jax.scipy.linalg.cho_solve((factor, True), proj)]
  transfers between devices with their start and end apart: 20 -> 6, of which waited for: 11 -> 4; matrix products, arithmetic and copies ran while one was open for 35% -> 4% of each run, Pallas kernels for 0% -> 12%
where the time goes in v1:
time: 311 us; the launch traced here: 310 us
  Pallas kernels  90.3 us (29%)
  waiting for transfers between devices  78.6 us (25%)
  blocking collectives  76.3 us (25%)
  local copies, waits for them, and re-layouts  36.6 us (12%)
  starting transfers between devices  27 us (9%)
    all_to_all x4, blocking collectives, exchange(): lax.all_to_all(value, WIDE_BLK, split_axis=0, concat_axis=0, tiled=True)  76.3 us
    ppermute x2, waiting for transfers between devices, sides(): after = lax.ppermute(value[:HALO], BLK, down)  71.7 us
    unnamed x36, local copies, waits for them, and re-layouts  25.3 us
    pallas_call x2, Pallas kernels, solve(): pl.pallas_call(solve_kernel, out_shape=[jax.ShapeDtypeStruct((WIDTH, WIDT...  19.6 us
    all_to_all x2, starting transfers between devices, exchange(): lax.all_to_all(value, WIDE_BLK, split_axis=0, concat_axis=0, tiled=True)  17.3 us
    pallas_call x1, Pallas kernels, near1(): pl.pallas_call(near1_kernel, grid=(rows // TILE,), in_specs=[whole(rows,...  16.8 us
    pallas_call x1, Pallas kernels, far0(): pl.pallas_call(far0_kernel, grid=(rows // TILE,), in_specs=[smem(), smem(...  15.3 us
    pallas_call x1, Pallas kernels, far1(): pl.pallas_call(far1_kernel, grid=(rows // TILE,), in_specs=[smem(), whole...  13.4 us
  transfers between devices with their start and end apart: 6, of which 4 were waited for; matrix products, arithmetic and copies ran while one was open for 4% of the time, Pallas kernels for 12%

profile of v1, /device:TPU:1, one launch (start us, length us, event | category | flops | bytes accessed | tf_op | source)
XLA Modules:
  0.0 309.6 jit_solution(13587434422266484743)
XLA Ops:
  5.0 8.4 %front.1 = bf16[128,64,256]{2,1,0:T(8,128)(2,1)S(1)} custom-call(s32[128]{0:T(128)S(1)} %bitcast.5, f32[4096,256]{1,0:T(8,128)S(1)} %copy-done, bf16[4096,64]{1,0:T(8,128)(2,1)S(1)} %copy.9.s), custom_call_target="tpu_custom_call" | custom-call | tf_op jit(solution)/shard_map/front/pallas_call | solution.py:87
  15.4 11.9 %all-to-all-start = ((bf16[128,64,256]{2,1,0:T(8,128)(2,1)}), bf16[128,64,256]{2,1,0:T(8,128)(2,1)}, u32[]{:S(2)}, u32[]{:S(2)}) async-start(bf16[128,64,256]{2,1,0:T(8,128)(2,1)} %copy-done.4), calls=%async_computation | async-start | bytes 8388608 | tf_op jit(solution)/shard_map/all_to_all | solution.py:464
  29.2 4.8 %collective-permute-start.1 = (f32[256,256]{1,0:T(8,128)}, f32[256,256]{1,0:T(8,128)S(1)}, u32[]{:S(2)}, u32[]{:S(2)}) collective-permute-start(f32[256,256]{1,0:T(8,128)} %get-tuple-element.38), channel_id=1, source_target_pairs={{1,0},{2,1},{3,2},{4,3},{5,4},{6,5},{7,6},{8,7},{9,8},{10,9},{11,1... | collective-permute-start | bytes 786440 | tf_op jit(solution)/shard_map/ppermute | solution.py:472
  34.5 4.9 %copy.10 = bf16[32,64,4,64]{3,2,1,0:T(4,128)(2,1)} copy(bf16[32,64,4,64]{3,1,2,0:T(8,128)(2,1)} %bitcast.7) | data formatting | bytes 2097152 | tf_op jit(solution)/shard_map/transpose | solution.py:480
  39.4 3.5 %reshape.15.coup = bf16[2048,256]{1,0:T(8,128)(2,1)S(1)} reshape(bf16[32,64,4,64]{3,2,1,0:T(4,128)(2,1)} %copy.10) | data formatting | bytes 2097152 | tf_op jit(solution)/shard_map/reshape | solution.py:480
  42.9 36.1 %collective-permute-done.1.hi = f32[256,256]{1,0:T(8,128)S(1)} collective-permute-done((f32[256,256]{1,0:T(8,128)}, f32[256,256]{1,0:T(8,128)S(1)}, u32[]{:S(2)}, u32[]{:S(2)}) %collective-permute-start.1) | collective-permute-done | bytes 262176 | tf_op jit(solution)/shard_map/ppermute | solution.py:472
  79.0 3.4 %collective-permute-done.lo = f32[256,256]{1,0:T(8,128)} collective-permute-done((f32[256,256]{1,0:T(8,128)}, f32[256,256]{1,0:T(8,128)}, u32[]{:S(2)}, u32[]{:S(2)}) %collective-permute-start) | collective-permute-done | bytes 262176 | tf_op jit(solution)/shard_map/ppermute | solution.py:471
  82.3 2.2 copy-done.1
  84.5 9.6 %near0.1 = (f32[4096,256]{1,0:T(8,128)S(1)}, f32[32,64,256]{2,1,0:T(8,128)S(1)}) custom-call(f32[4096,256]{1,0:T(8,128)S(1)} %copy-done.1, f32[256,256]{1,0:T(8,128)} %collective-permute-done.lo, f32[256,256]{1,0:T(8,128)S(1)} %collective-permute-done.1.hi, bf16[4096,1536]{1,0:T(8,128)(2,1)} %near.3, bf16[4096,64]{1,0:T(8,128)(2,1)S(1)} %copy.9.s), custom_call_target="tpu_custom_call" | custom-call | flops 4000000000 | bytes 24000000 | tf_op jit(solution)/shard_map/near0/pallas_call | solution.py:126
  99.1 15.3 %far0.1 = (f32[4096,256]{1,0:T(8,128)S(1)}, f32[2048,256]{1,0:T(8,128)S(1)}, f32[128,8,128]{2,1,0:T(8,128)S(1)}, bf16[128,64,256]{2,1,0:T(8,128)(2,1)}) custom-call(s32[128]{0:T(128)S(1)} %bitcast.6, s32[128]{0:T(128)S(1)} %bitcast.3, bf16[128,64,256]{2,1,0:T(8,128)(2,1)} %all-to-all-done.incoming, bf16[2048,256]{1,0:T(8,128)(2,1)S(1)} %reshape.15.coup, ...), custom_call_target="tpu_custom_call" | custom-call | tf_op jit(solution)/shard_map/far0/pallas_call | solution.py:211
  117.8 20.2 %all_to_all.30.parts = f32[128,8,128]{2,1,0:T(8,128)S(1)} all-to-all(f32[128,8,128]{2,1,0:T(8,128)S(1)} %get-tuple-element.22), channel_id=1, replica_groups=mesh['wide_0'=4,'wide_1'=2,'blk_0'=4,'blk_1'=4] {'wide_0','wide_1','blk_..., dimensions={0} | all-to-all | bytes 1048576 | tf_op jit(solution)/shard_map/all_to_all | solution.py:464
  138.2 17.9 %all_to_all.31.gp = f32[128,8,128]{2,1,0:T(8,128)S(1)} all-to-all(f32[128,8,128]{2,1,0:T(8,128)S(1)} %summed.2), channel_id=1, replica_groups=mesh['wide_0'=4,'wide_1'=2,'blk_0'=4,'blk_1'=4] {'wide_0','wide_1','blk_..., dimensions={0} | all-to-all | bytes 1048576 | tf_op jit(solution)/shard_map/all_to_all | solution.py:464
  156.1 5.3 %all-to-all-start.3 = ((bf16[128,64,256]{2,1,0:T(8,128)(2,1)}), bf16[128,64,256]{2,1,0:T(8,128)(2,1)}, u32[]{:S(2)}, u32[]{:S(2)}) async-start(bf16[128,64,256]{2,1,0:T(8,128)(2,1)} %get-tuple-element.29), calls=%async_computation.3 | async-start | bytes 8388608 | tf_op jit(solution)/shard_map/all_to_all | solution.py:464
  162.4 5.0 %collective-permute-start.3 = (f32[256,256]{1,0:T(8,128)S(1)}, f32[256,256]{1,0:T(8,128)S(1)}, u32[]{:S(2)}, u32[]{:S(2)}) collective-permute-start(f32[256,256]{1,0:T(8,128)S(1)} %get-tuple-element.36), channel_id=1, source_target_pairs={{1,0},{2,1},{3,2},{4,3},{5,4},{6,5},{7,6},{8,7},{9,8},{10,9},{11,1... | collective-permute-start | bytes 786440 | tf_op jit(solution)/shard_map/ppermute | solution.py:472
  167.4 9.8 %solve.2 = (f32[256,256]{1,0:T(8,128)}, bf16[256,256]{1,0:T(8,128)(2,1)S(1)}, bf16[256,256]{1,0:T(8,128)(2,1)S(1)}) custom-call(f32[128,8,128]{2,1,0:T(8,128)S(1)} %all_to_all.31.gp), custom_call_target="tpu_custom_call" | custom-call | flops 12000000000 | bytes 1000000 | tf_op jit(solution)/shard_map/solve/pallas_call | solution.py:325
  177.3 35.7 %collective-permute-done.3.ihi = f32[256,256]{1,0:T(8,128)S(1)} collective-permute-done((f32[256,256]{1,0:T(8,128)S(1)}, f32[256,256]{1,0:T(8,128)S(1)}, u32[]{:S(2)}, u32[]{:S(2)}) %collective-permute-start.3) | collective-permute-done | bytes 262176 | tf_op jit(solution)/shard_map/ppermute | solution.py:472
  212.9 3.5 %collective-permute-done.2.ilo = f32[256,256]{1,0:T(8,128)S(1)} collective-permute-done((f32[256,256]{1,0:T(8,128)S(1)}, f32[256,256]{1,0:T(8,128)S(1)}, u32[]{:S(2)}, u32[]{:S(2)}) %collective-permute-start.2) | collective-permute-done | bytes 262176 | tf_op jit(solution)/shard_map/ppermute | solution.py:471
  216.4 16.8 %near1.1 = (f32[4096,256]{1,0:T(8,128)S(1)}, f32[4096,256]{1,0:T(8,128)}, f32[4096,256]{1,0:T(8,128)}) custom-call(f32[4096,256]{1,0:T(8,128)} %r.7, f32[256,256]{1,0:T(8,128)} %collective-permute-done.lo, f32[256,256]{1,0:T(8,128)S(1)} %collective-permute-done.1.hi, f32[4096,256]{1,0:T(8,128)} %copy-done.12, f32[256,256]{1,0:T(8,128)S(1)} %collective-permute-done.2.ilo, ...), custom_call_target="tpu_custom_call" | custom-call | flops 8000000000 | bytes 36000000 | tf_op jit(solution)/shard_map/near1/pallas_call | solution.py:363
  235.3 2.2 copy-done.3
  241.2 13.4 %far1.1 = (f32[4096,256]{1,0:T(8,128)S(1)}, f32[128,8,128]{2,1,0:T(8,128)S(1)}) custom-call(s32[128]{0:T(128)S(1)} %bitcast.4, bf16[128,64,256]{2,1,0:T(8,128)(2,1)} %all-to-all-done.3.incoming, bf16[2048,256]{1,0:T(8,128)(2,1)S(1)} %reshape.15.coup, bf16[4096,64]{1,0:T(8,128)(2,1)S(1)} %copy.12.tb, f32[4096,256]{1,0:T(8,128)S(1)} %copy-done.6, ...), custom_call_target="tpu_custom_call" | custom-call | tf_op jit(solution)/shard_map/far1/pallas_call | solution.py:417
  254.7 20.3 %all_to_all.32.parts = f32[128,8,128]{2,1,0:T(8,128)S(1)} all-to-all(f32[128,8,128]{2,1,0:T(8,128)S(1)} %get-tuple-element.33), channel_id=1, replica_groups=mesh['wide_0'=4,'wide_1'=2,'blk_0'=4,'blk_1'=4] {'wide_0','wide_1','blk_..., dimensions={0} | all-to-all | bytes 1048576 | tf_op jit(solution)/shard_map/all_to_all | solution.py:464
  275.2 17.9 %all_to_all.33.gp = f32[128,8,128]{2,1,0:T(8,128)S(1)} all-to-all(f32[128,8,128]{2,1,0:T(8,128)S(1)} %summed.3), channel_id=1, replica_groups=mesh['wide_0'=4,'wide_1'=2,'blk_0'=4,'blk_1'=4] {'wide_0','wide_1','blk_..., dimensions={0} | all-to-all | bytes 1048576 | tf_op jit(solution)/shard_map/all_to_all | solution.py:464
  293.1 9.8 %solve.3 = (f32[256,256]{1,0:T(8,128)}, bf16[256,256]{1,0:T(8,128)(2,1)S(1)}, bf16[256,256]{1,0:T(8,128)(2,1)S(1)}) custom-call(f32[128,8,128]{2,1,0:T(8,128)S(1)} %all_to_all.33.gp), custom_call_target="tpu_custom_call" | custom-call | flops 12000000000 | bytes 1000000 | tf_op jit(solution)/shard_map/solve/pallas_call | solution.py:325
  302.9 6.7 %finish.1 = (f32[4096,256]{1,0:T(8,128)}, f32[4096,256]{1,0:T(8,128)}) custom-call(f32[4096,256]{1,0:T(8,128)S(1)} %copy-done.5, f32[4096,256]{1,0:T(8,128)S(1)} %copy-done.3, f32[4096,256]{1,0:T(8,128)S(1)} %get-tuple-element.32.image, bf16[256,256]{1,0:T(8,128)(2,1)S(1)} %get-tuple-element.34.ah, bf16[256,256]{1,0:T(8,128)(2,1)S(1)} %get-tuple-element.35.al), custom_call_target="tpu_custom_call" | custom-call | tf_op jit(solution)/shard_map/finish/pallas_call | solution.py:452
  (42 shorter events, 24.2 us)
Async XLA Ops:
  2.2 2.2 copy-start
  4.3 0.7 copy-start.14
  13.4 2.0 copy-start.4
  15.4 18.6 %copy-start.16 = (bf16[4096,64]{0,1:T(8,128)(2,1)S(1)}, bf16[4096,64]{0,1:T(8,128)(2,1)}, u32[]{:S(2)}) copy-start(bf16[4096,64]{0,1:T(8,128)(2,1)} %param.10) | copy-start | bytes 1572868
  15.4 82.1 %all-to-all-start = ((bf16[128,64,256]{2,1,0:T(8,128)(2,1)}), bf16[128,64,256]{2,1,0:T(8,128)(2,1)}, u32[]{:S(2)}, u32[]{:S(2)}) async-start(bf16[128,64,256]{2,1,0:T(8,128)(2,1)} %copy-done.4), calls=%async_computation | async-start | bytes 8388608 | tf_op jit(solution)/shard_map/all_to_all | solution.py:464
  29.2 49.7 %collective-permute-start.1 = (f32[256,256]{1,0:T(8,128)}, f32[256,256]{1,0:T(8,128)S(1)}, u32[]{:S(2)}, u32[]{:S(2)}) collective-permute-start(f32[256,256]{1,0:T(8,128)} %get-tuple-element.38), channel_id=1, source_target_pairs={{1,0},{2,1},{3,2},{4,3},{5,4},{6,5},{7,6},{8,7},{9,8},{10,9},{11,1... | collective-permute-start | bytes 786440 | tf_op jit(solution)/shard_map/ppermute | solution.py:472
  34.0 48.3 %collective-permute-start = (f32[256,256]{1,0:T(8,128)}, f32[256,256]{1,0:T(8,128)}, u32[]{:S(2)}, u32[]{:S(2)}) collective-permute-start(f32[256,256]{1,0:T(8,128)} %get-tuple-element.39), channel_id=1, source_target_pairs={{0,1},{1,2},{2,3},{3,4},{4,5},{5,6},{6,7},{7,8},{8,9},{9,10},{10,1... | collective-permute-start | bytes 786440 | tf_op jit(solution)/shard_map/ppermute | solution.py:471
  39.4 58.2 %copy-start.13 = (s32[1,128]{1,0:T(1,128)S(1)}, s32[1,128]{1,0:T(1,128)}, u32[]{:S(2)}) copy-start(s32[1,128]{1,0:T(1,128)} %param.13) | copy-start | bytes 1540
  39.4 58.2 %copy-start.15 = (s32[1,128,1]{1,2,0:T(1,128)S(1)}, s32[1,128,1]{1,2,0:T(1,128)}, u32[]{:S(2)}) copy-start(s32[1,128,1]{1,2,0:T(1,128)} %param.12) | copy-start | bytes 1540
  82.3 2.2 copy-start.1
  94.1 2.0 copy-start.7
  96.1 1.4 copy-start.10
  97.5 1.6 copy-start.11
  114.5 1.3 copy-start.8
  115.8 2.0 copy-start.12
  156.1 79.2 %all-to-all-start.3 = ((bf16[128,64,256]{2,1,0:T(8,128)(2,1)}), bf16[128,64,256]{2,1,0:T(8,128)(2,1)}, u32[]{:S(2)}, u32[]{:S(2)}) async-start(bf16[128,64,256]{2,1,0:T(8,128)(2,1)} %get-tuple-element.29), calls=%async_computation.3 | async-start | bytes 8388608 | tf_op jit(solution)/shard_map/all_to_all | solution.py:464
  162.4 50.5 %collective-permute-start.3 = (f32[256,256]{1,0:T(8,128)S(1)}, f32[256,256]{1,0:T(8,128)S(1)}, u32[]{:S(2)}, u32[]{:S(2)}) collective-permute-start(f32[256,256]{1,0:T(8,128)S(1)} %get-tuple-element.36), channel_id=1, source_target_pairs={{1,0},{2,1},{3,2},{4,3},{5,4},{6,5},{7,6},{8,7},{9,8},{10,9},{11,1... | collective-permute-start | bytes 786440 | tf_op jit(solution)/shard_map/ppermute | solution.py:472
  167.4 49.0 %collective-permute-start.2 = (f32[256,256]{1,0:T(8,128)S(1)}, f32[256,256]{1,0:T(8,128)S(1)}, u32[]{:S(2)}, u32[]{:S(2)}) collective-permute-start(f32[256,256]{1,0:T(8,128)S(1)} %get-tuple-element.37), channel_id=1, source_target_pairs={{0,1},{1,2},{2,3},{3,4},{4,5},{5,6},{6,7},{7,8},{8,9},{9,10},{10,1... | collective-permute-start | bytes 786440 | tf_op jit(solution)/shard_map/ppermute | solution.py:471
  233.2 2.0 copy-start.2
  235.3 2.2 copy-start.3
  237.4 2.2 copy-start.6
  239.6 1.6 copy-start.9
  293.1 9.8 %copy-start.5 = (f32[4096,256]{1,0:T(8,128)S(1)}, f32[4096,256]{1,0:T(8,128)}, u32[]{:S(2)}) copy-start(f32[4096,256]{1,0:T(8,128)} %get-tuple-element.27.sol) | copy-start | bytes 12582916

commit v2 on v1

--- a/solution.py
+++ b/solution.py
@@ -12,6 +12,7 @@
 RANK = 64
 WIDTH = 256
 TILE = 512
+FULL = 58
 BLK = ("blk_0", "blk_1")
 WIDE_BLK = ("wide_0", "wide_1", "blk_0", "blk_1")
 F32 = jnp.float32
@@ -31,6 +32,10 @@
 
 def tiled(*shape):
     return pl.BlockSpec(shape, lambda t: (t,) + (0,) * (len(shape) - 1))
+
+
+def across(rows, cols):
+    return pl.BlockSpec((rows, cols), lambda t: (0, t))
 
 
 def smem():
@@ -74,7 +79,7 @@
     per = TILE // LEAF
     for i in range(per):
         rows = slice(i * LEAF, (i + 1) * LEAF)
-        packed[t * per + i] = dot_t(s[rows], vb[rows]).astype(BF16)
+        packed[t * per + i] = dot(s[:, rows], vb[rows]).astype(BF16)
 
     @pl.when(t == pl.num_programs(0) - 1)
     def _():
@@ -87,27 +92,27 @@
     return pl.pallas_call(
         front_kernel,
         grid=(rows // TILE,),
-        in_specs=[smem(), tiled(TILE, WIDTH), tiled(TILE, RANK)],
+        in_specs=[smem(), tiled(TILE, WIDTH), across(RANK, TILE)],
         out_specs=hbm(),
         out_shape=jax.ShapeDtypeStruct((count, RANK, WIDTH), BF16),
         scratch_shapes=[
             pltpu.VMEM((rows // LEAF, RANK, WIDTH), BF16),
             pltpu.SemaphoreType.DMA(()),
         ],
-        compiler_params=params(16),
+        compiler_params=params(FULL),
         name="front",
     )(ids, r, s)
 
 
-def near0_kernel(r, lo, hi, near, s, base, err, ext):
+def near0_kernel(r, near, s, base, err, ext):
     t = pl.program_id(0)
     rows = r.shape[0]
 
     @pl.when(t == 0)
     def _():
-        ext[:HALO] = lo[...].astype(BF16)
+        ext[:HALO] = jnp.zeros((HALO, WIDTH), BF16)
         ext[HALO : HALO + rows] = r[...].astype(BF16)
-        ext[HALO + rows :] = hi[...].astype(BF16)
+        ext[HALO + rows :] = jnp.zeros((HALO, WIDTH), BF16)
 
     first = pl.multiple_of((t // (NEAR // TILE)) * NEAR, NEAR)
     own = r[pl.ds(pl.multiple_of(t * TILE, TILE), TILE)]
@@ -115,12 +120,12 @@
     rh, rl = halves(own)
     for i in range(TILE // LEAF):
         cut = slice(i * LEAF, (i + 1) * LEAF)
-        high = dot_t(s[cut], rh[cut])
-        low = dot_t(s[cut], rl[cut])
+        high = dot(s[:, cut], rh[cut])
+        low = dot(s[:, cut], rl[cut])
         err[i] = (high.astype(BF16).astype(F32) - high) - low
 
 
-def near0(r, lo, hi, near, s):
+def near0(r, near, s):
     rows = r.shape[0]
     per = TILE // LEAF
     return pl.pallas_call(
@@ -128,10 +133,8 @@
         grid=(rows // TILE,),
         in_specs=[
             whole(rows, WIDTH),
-            whole(HALO, WIDTH),
-            whole(HALO, WIDTH),
             tiled(TILE, NEAR + 2 * HALO),
-            tiled(TILE, RANK),
+            across(RANK, TILE),
         ],
         out_specs=[tiled(TILE, WIDTH), tiled(per, RANK, WIDTH)],
         out_shape=[
@@ -139,10 +142,10 @@
             jax.ShapeDtypeStruct((rows // LEAF, RANK, WIDTH), F32),
         ],
         scratch_shapes=[pltpu.VMEM((rows + 2 * HALO, WIDTH), BF16)],
-        compiler_params=params(32),
+        compiler_params=params(FULL),
         cost_estimate=pl.CostEstimate(flops=4_000_000_000, bytes_accessed=24_000_000, transcendentals=0),
         name="near0",
-    )(r, lo, hi, near, s)
+    )(r, near, s)
 
 
 def gram_step(t, image, r, acc):
@@ -173,7 +176,29 @@
     return jnp.concatenate([incoming[readers[leaf * 4 + f]] for f in range(4)], axis=0)
 
 
-def far0_kernel(ids, readers, incoming, coup, tb, s, base, r, err, image, trans, gp, out, packed, direct, acc, sem):
+def edge_specs(tiles):
+    edge = NEAR // TILE
+    return [
+        whole(HALO, WIDTH),
+        whole(HALO, WIDTH),
+        pl.BlockSpec((TILE, HALO), lambda t: (jnp.minimum(t, edge - 1), 0)),
+        pl.BlockSpec((TILE, HALO), lambda t: (jnp.maximum(t, tiles - edge), (NEAR + HALO) // HALO)),
+    ]
+
+
+def add_edges(t, image, first, last, left, right):
+    edge = NEAR // TILE
+
+    @pl.when(t < edge)
+    def _():
+        image[...] += dot(left[...], first())
+
+    @pl.when(t >= pl.num_programs(0) - edge)
+    def _():
+        image[...] += dot(right[...], last())
+
+
+def far0_kernel(ids, readers, incoming, coup, tb, s, base, r, err, lo, hi, left, right, image, first, last, trans, gp, out, packed, direct, acc, sem):
     t = pl.program_id(0)
     per = TILE // LEAF
     tiles = []
@@ -182,12 +207,21 @@
         tr = dot(coup[i * RANK : (i + 1) * RANK], slots_of(readers, incoming, t * per + i))
         trans[i * RANK : (i + 1) * RANK] = tr
         tiles.append(base[cut] + dot(tb[cut], tr.astype(BF16)))
-    value = jnp.concatenate(tiles, axis=0)
-    image[...] = value
-    ih, il = gram_step(t, value, r[...], acc)
+    image[...] = jnp.concatenate(tiles, axis=0)
+    add_edges(t, image, lambda: lo[...].astype(BF16), lambda: hi[...].astype(BF16), left, right)
+
+    @pl.when(t == 0)
+    def _():
+        first[...] = image[:HALO]
+
+    @pl.when(t == pl.num_programs(0) - 1)
+    def _():
+        last[...] = image[TILE - HALO :]
+
+    ih, il = gram_step(t, image[...], r[...], acc)
     for i in range(per):
         cut = slice(i * LEAF, (i + 1) * LEAF)
-        direct[t * per + i] = dot_t(s[cut], ih[cut]) + dot_t(s[cut], il[cut])
+        direct[t * per + i] = dot(s[:, cut], ih[cut]) + dot(s[:, cut], il[cut])
 
     @pl.when(t == pl.num_programs(0) - 1)
     def _():
@@ -203,7 +237,7 @@
         send_rows(packed, ids, out, sem, out.shape[0])
 
 
-def far0(ids, readers, incoming, coup, tb, s, base, r, err):
+def far0(ids, readers, incoming, coup, tb, s, base, r, err, lo, hi, near):
     rows = r.shape[0]
     leaves = rows // LEAF
     count = ids.shape[0]
@@ -217,14 +251,24 @@
             whole(count, RANK, WIDTH),
             tiled(per * RANK, 4 * RANK),
             tiled(TILE, RANK),
-            tiled(TILE, RANK),
+            across(RANK, TILE),
             tiled(TILE, WIDTH),
             tiled(TILE, WIDTH),
             whole(leaves, RANK, WIDTH),
-        ],
-        out_specs=[tiled(TILE, WIDTH), tiled(per * RANK, WIDTH), whole(128, 8, 128), hbm()],
+            *edge_specs(rows // TILE),
+        ],
+        out_specs=[
+            tiled(TILE, WIDTH),
+            whole(HALO, WIDTH),
+            whole(HALO, WIDTH),
+            tiled(per * RANK, WIDTH),
+            whole(128, 8, 128),
+            hbm(),
+        ],
         out_shape=[
             jax.ShapeDtypeStruct((rows, WIDTH), F32),
+            jax.ShapeDtypeStruct((HALO, WIDTH), F32),
+            jax.ShapeDtypeStruct((HALO, WIDTH), F32),
             jax.ShapeDtypeStruct((leaves * RANK, WIDTH), F32),
             jax.ShapeDtypeStruct((128, 8, 128), F32),
             jax.ShapeDtypeStruct((count, RANK, WIDTH), BF16),
@@ -235,9 +279,9 @@
             pltpu.VMEM((WIDTH, 2 * WIDTH), F32),
             pltpu.SemaphoreType.DMA(()),
         ],
-        compiler_params=params(40),
+        compiler_params=params(FULL),
         name="far0",
-    )(ids, readers, incoming, coup, tb, s, base, r, err)
+    )(ids, readers, incoming, coup, tb, s, base, r, err, lo, hi, near, near)
 
 
 def sum_kernel(parts, out):
@@ -335,20 +379,20 @@
     )(gp)
 
 
-def near1_kernel(r, lo, hi, image, ilo, ihi, ah, al, near, resid, base, sol, ext, full):
+def near1_kernel(r, image, ah, al, near, resid, base, sol, ext, full):
     t = pl.program_id(0)
     rows = r.shape[0]
     high, low = ah[...], al[...]
 
     @pl.when(t == 0)
     def _():
-        ext[:HALO] = (lo[...] - dot3(ilo[...], high, low)).astype(BF16)
+        ext[:HALO] = jnp.zeros((HALO, WIDTH), BF16)
         for c in range(rows // TILE):
             cut = slice(c * TILE, (c + 1) * TILE)
             value = r[cut] - dot3(image[cut], high, low)
             full[cut] = value
             ext[HALO + c * TILE : HALO + (c + 1) * TILE] = value.astype(BF16)
-        ext[HALO + rows :] = (hi[...] - dot3(ihi[...], high, low)).astype(BF16)
+        ext[HALO + rows :] = jnp.zeros((HALO, WIDTH), BF16)
 
     first = pl.multiple_of((t // (NEAR // TILE)) * NEAR, NEAR)
     here = pl.ds(pl.multiple_of(t * TILE, TILE), TILE)
@@ -358,18 +402,14 @@
     sol[...] = dot3(r[here], high, low)
 
 
-def near1(r, lo, hi, image, ilo, ihi, ah, al, near):
+def near1(r, image, ah, al, near):
     rows = r.shape[0]
     return pl.pallas_call(
         near1_kernel,
         grid=(rows // TILE,),
         in_specs=[
             whole(rows, WIDTH),
-            whole(HALO, WIDTH),
-            whole(HALO, WIDTH),
             whole(rows, WIDTH),
-            whole(HALO, WIDTH),
-            whole(HALO, WIDTH),
             whole(WIDTH, WIDTH),
             whole(WIDTH, WIDTH),
             tiled(TILE, NEAR + 2 * HALO),
@@ -380,13 +420,13 @@
             pltpu.VMEM((rows + 2 * HALO, WIDTH), BF16),
             pltpu.VMEM((rows, WIDTH), F32),
         ],
-        compiler_params=params(48),
+        compiler_params=params(FULL),
         cost_estimate=pl.CostEstimate(flops=8_000_000_000, bytes_accessed=36_000_000, transcendentals=0),
         name="near1",
-    )(r, lo, hi, image, ilo, ihi, ah, al, near)
-
-
-def far1_kernel(readers, incoming, coup, tb, base, r, trans, ah, al, image, gp, acc):
+    )(r, image, ah, al, near)
+
+
+def far1_kernel(readers, incoming, coup, tb, base, r, trans, ah, al, lo, hi, ilo, ihi, left, right, image, gp, acc):
     t = pl.program_id(0)
     per = TILE // LEAF
     moved = jnp.concatenate(
@@ -401,16 +441,23 @@
     for i in range(per):
         cut = slice(i * LEAF, (i + 1) * LEAF)
         tiles.append(base[cut] + dot(tb[cut], tr[i * RANK : (i + 1) * RANK]))
-    value = jnp.concatenate(tiles, axis=0)
-    image[...] = value
-    gram_step(t, value, r[...], acc)
+    image[...] = jnp.concatenate(tiles, axis=0)
+    add_edges(
+        t,
+        image,
+        lambda: (lo[...] - dot3(ilo[...], ah[...], al[...])).astype(BF16),
+        lambda: (hi[...] - dot3(ihi[...], ah[...], al[...])).astype(BF16),
+        left,
+        right,
+    )
+    gram_step(t, image[...], r[...], acc)
 
     @pl.when(t == pl.num_programs(0) - 1)
     def _():
         gram_end(acc, gp)
 
 
-def far1(readers, incoming, coup, tb, base, r, trans, ah, al):
+def far1(readers, incoming, coup, tb, base, r, trans, ah, al, lo, hi, ilo, ihi, near):
     rows = r.shape[0]
     count = incoming.shape[0]
     per = TILE // LEAF
@@ -427,6 +474,9 @@
             tiled(per * RANK, WIDTH),
             whole(WIDTH, WIDTH),
             whole(WIDTH, WIDTH),
+            whole(HALO, WIDTH),
+            whole(HALO, WIDTH),
+            *edge_specs(rows // TILE),
         ],
         out_specs=[tiled(TILE, WIDTH), whole(128, 8, 128)],
         out_shape=[
@@ -436,9 +486,9 @@
         scratch_shapes=[
             pltpu.VMEM((WIDTH, 2 * WIDTH), F32),
         ],
-        compiler_params=params(32),
+        compiler_params=params(FULL),
         name="far1",
-    )(readers, incoming, coup, tb, base, r, trans, ah, al)
+    )(readers, incoming, coup, tb, base, r, trans, ah, al, lo, hi, ilo, ihi, near, near)
 
 
 def finish_kernel(sol, r, image, ah, al, solution, residual):
@@ -455,7 +505,7 @@
         in_specs=[tiled(TILE, WIDTH)] * 3 + [whole(WIDTH, WIDTH)] * 2,
         out_specs=[tiled(TILE, WIDTH)] * 2,
         out_shape=[jax.ShapeDtypeStruct((rows, WIDTH), F32)] * 2,
-        compiler_params=params(16),
+        compiler_params=params(FULL),
         name="finish",
     )(sol, r, image, ah, al)
 
@@ -464,35 +514,35 @@
     return lax.all_to_all(value, WIDE_BLK, split_axis=0, concat_axis=0, tiled=True)
 
 
-def sides(value):
+def sides(first, last):
     count = lax.axis_size(BLK)
     up = [(i, (i + 1) % count) for i in range(count)]
     down = [(j, i) for i, j in up]
-    before = lax.ppermute(value[-HALO:], BLK, up)
-    after = lax.ppermute(value[:HALO], BLK, down)
-    return before, after
+    return lax.ppermute(last, BLK, up), lax.ppermute(first, BLK, down)
 
 
 def shards(rhs, near_blocks, source_basis, target_basis, far_coupling, send_ids, far_list):
     leaves = rhs.shape[0] // LEAF
     ids = send_ids.reshape(-1)
     readers = far_list.reshape(-1)
+    source = source_basis.T
+    incoming = exchange(front(ids, rhs, source))
     coup = far_coupling.transpose(0, 2, 1, 3).reshape(leaves * RANK, 4 * RANK)
-    lo, hi = sides(rhs)
-    incoming = exchange(front(ids, rhs, source_basis))
-    base0, err = near0(rhs, lo, hi, near_blocks, source_basis)
-    image0, trans0, gp0, outgoing = far0(
-        ids, readers, incoming, coup, target_basis, source_basis, base0, rhs, err
+    lo, hi = sides(rhs[:HALO], rhs[-HALO:])
+    base0, err = near0(rhs, near_blocks, source)
+    image0, first0, last0, trans0, gp0, outgoing = far0(
+        ids, readers, incoming, coup, target_basis, source, base0, rhs, err, lo, hi, near_blocks
     )
-    parts = exchange(gp0)
-    ilo, ihi = sides(image0)
-    total = summed(parts)
+    total = summed(exchange(gp0))
     total, outgoing = lax.optimization_barrier((total, outgoing))
     whole0 = exchange(total)
     incoming1 = exchange(outgoing)
+    ilo, ihi = sides(first0, last0)
     _, ah, al = solve(whole0)
-    r1, base1, sol = near1(rhs, lo, hi, image0, ilo, ihi, ah, al, near_blocks)
-    image1, gp1 = far1(readers, incoming1, coup, target_basis, base1, r1, trans0, ah, al)
+    r1, base1, sol = near1(rhs, image0, ah, al, near_blocks)
+    image1, gp1 = far1(
+        readers, incoming1, coup, target_basis, base1, r1, trans0, ah, al, lo, hi, ilo, ihi, near_blocks
+    )
     whole1 = exchange(summed(exchange(gp1)))
     _, bh, bl = solve(whole1)
     return tuple(finish(sol, r1, image1, bh, bl))

time: 311 us -> 278 us (0.89)
  waiting for transfers between devices: 78.6 us -> 49 us
  local copies, waits for them, and re-layouts: 36.6 us -> 13.1 us
  Pallas kernels: 90.3 us -> 110 us
    ppermute x4, waiting for transfers between devices: 78.6 us -> 48.9 us  [sides(): return (lax.ppermute(last, BLK, up), lax.ppermute(first, BLK, down))]
    unnamed x36 -> x23, local copies, waits for them, and re-layouts: 25.3 us -> 5.51 us
    pallas_call x1, Pallas kernels: 13.4 us -> 19.5 us  [far1(): pl.pallas_call(far1_kernel, grid=(rows // TILE,), in_specs=[smem(), whole...]
    pallas_call x1, Pallas kernels: 6.74 us -> 11.8 us  [finish(): pl.pallas_call(finish_kernel, grid=(rows // TILE,), in_specs=[tiled(TILE,...]
    pallas_call x1, Pallas kernels: 15.3 us -> 20.2 us  [far0(): pl.pallas_call(far0_kernel, grid=(rows // TILE,), in_specs=[smem(), smem(...]
    pallas_call x1, Pallas kernels: 9.59 us -> 12.8 us  [near0(): pl.pallas_call(near0_kernel, grid=(rows // TILE,), in_specs=[whole(rows,...]
  transfers between devices with their start and end apart: 6 -> 6, of which waited for: 4 -> 2; matrix products, arithmetic and copies ran while one was open for 4% -> 3% of each run, Pallas kernels for 12% -> 15%
where the time goes in v2:
time: 278 us; the launch traced here: 276 us
  Pallas kernels  110 us (40%)
  blocking collectives  76.7 us (28%)
  waiting for transfers between devices  49 us (18%)
  starting transfers between devices  27.4 us (10%)
  local copies, waits for them, and re-layouts  13.1 us (5%)
    all_to_all x4, blocking collectives, exchange(): lax.all_to_all(value, WIDE_BLK, split_axis=0, concat_axis=0, tiled=True)  76.7 us
    ppermute x4, waiting for transfers between devices, sides(): return (lax.ppermute(last, BLK, up), lax.ppermute(first, BLK, down))  48.9 us
    pallas_call x1, Pallas kernels, far0(): pl.pallas_call(far0_kernel, grid=(rows // TILE,), in_specs=[smem(), smem(...  20.2 us
    pallas_call x2, Pallas kernels, solve(): pl.pallas_call(solve_kernel, out_shape=[jax.ShapeDtypeStruct((WIDTH, WIDT...  19.6 us
    pallas_call x1, Pallas kernels, far1(): pl.pallas_call(far1_kernel, grid=(rows // TILE,), in_specs=[smem(), whole...  19.5 us
    pallas_call x1, Pallas kernels, near1(): pl.pallas_call(near1_kernel, grid=(rows // TILE,), in_specs=[whole(rows,...  18.1 us
    all_to_all x2, starting transfers between devices, exchange(): lax.all_to_all(value, WIDE_BLK, split_axis=0, concat_axis=0, tiled=True)  17.4 us
    pallas_call x1, Pallas kernels, near0(): pl.pallas_call(near0_kernel, grid=(rows // TILE,), in_specs=[whole(rows,...  12.8 us
  transfers between devices with their start and end apart: 6, of which 2 were waited for; matrix products, arithmetic and copies ran while one was open for 3% of the time, Pallas kernels for 15%

profile of v2, /device:TPU:1, one launch (start us, length us, event | category | flops | bytes accessed | tf_op | source)
XLA Modules:
  0.0 276.4 jit_solution(2626118840535012911)
XLA Ops:
  0.6 7.2 %front.1 = bf16[128,64,256]{2,1,0:T(8,128)(2,1)} custom-call(s32[128]{0:T(128)} %bitcast.8, f32[4096,256]{1,0:T(8,128)} %r.7, bf16[64,4096]{1,0:T(8,128)(2,1)} %bitcast.4), custom_call_target="tpu_custom_call" | custom-call | tf_op jit(solution)/shard_map/front/pallas_call | solution.py:92
  7.9 12.0 %all-to-all-start = ((bf16[128,64,256]{2,1,0:T(8,128)(2,1)}), bf16[128,64,256]{2,1,0:T(8,128)(2,1)}, u32[]{:S(2)}, u32[]{:S(2)}) async-start(bf16[128,64,256]{2,1,0:T(8,128)(2,1)} %front.1), calls=%async_computation | async-start | bytes 8388608 | tf_op jit(solution)/shard_map/all_to_all | solution.py:514
  19.8 1.8 fusion
  21.7 1.4 collective-permute-start
  23.0 3.4 %collective-permute-start.1 = (f32[256,256]{1,0:T(8,128)S(1)}, f32[256,256]{1,0:T(8,128)S(1)}, u32[]{:S(2)}, u32[]{:S(2)}) collective-permute-start(f32[256,256]{1,0:T(8,128)S(1)} %get-tuple-element.40), channel_id=1, source_target_pairs={{1,0},{2,1},{3,2},{4,3},{5,4},{6,5},{7,6},{8,7},{9,8},{10,9},{11,1... | collective-permute-start | bytes 786440 | tf_op jit(solution)/shard_map/ppermute | solution.py:521
  26.5 3.6 %copy.9 = bf16[32,64,4,64]{3,2,1,0:T(4,128)(2,1)S(1)} copy(bf16[32,64,4,64]{3,1,2,0:T(8,128)(2,1)} %bitcast.7) | data formatting | bytes 2097152 | tf_op jit(solution)/shard_map/transpose | solution.py:530
  30.0 2.1 reshape.15.coup
  32.2 1.3 copy.10.tb
  33.5 12.8 %near0.1 = (f32[4096,256]{1,0:T(8,128)}, f32[32,64,256]{2,1,0:T(8,128)}) custom-call(f32[4096,256]{1,0:T(8,128)} %r.7, bf16[4096,1536]{1,0:T(8,128)(2,1)} %right.3, bf16[64,4096]{1,0:T(8,128)(2,1)} %bitcast.5), custom_call_target="tpu_custom_call" | custom-call | flops 4000000000 | bytes 24000000 | tf_op jit(solution)/shard_map/near0/pallas_call | solution.py:131
  46.3 28.5 %collective-permute-done.lo = f32[256,256]{1,0:T(8,128)S(1)} collective-permute-done((f32[256,256]{1,0:T(8,128)}, f32[256,256]{1,0:T(8,128)S(1)}, u32[]{:S(2)}, u32[]{:S(2)}) %collective-permute-start) | collective-permute-done | bytes 262176 | tf_op jit(solution)/shard_map/ppermute | solution.py:521
  75.5 20.2 %far0.1 = (f32[4096,256]{1,0:T(8,128)}, f32[256,256]{1,0:T(8,128)}, f32[256,256]{1,0:T(8,128)}, f32[2048,256]{1,0:T(8,128)}, f32[128,8,128]{2,1,0:T(8,128)}, /*index=5*/bf16[128,64,256]{2,1,0:T(8,128)(2,1)}) custom-call(s32[128]{0:T(128)} %bitcast.9, s32[128]{0:T(128)} %bitcast.10, bf16[128,64,256]{2,1,0:T(8,128)(2,1)} %all-to-all-done.incoming, ...), custom_call_target="tpu_custom_call" | custom-call | tf_op jit(solution)/shard_map/far0/pallas_call | solution.py:245
  95.7 20.5 %all_to_all.30.parts = f32[128,8,128]{2,1,0:T(8,128)S(1)} all-to-all(f32[128,8,128]{2,1,0:T(8,128)} %get-tuple-element.24), channel_id=1, replica_groups=mesh['wide_0'=4,'wide_1'=2,'blk_0'=4,'blk_1'=4] {'wide_0','wide_1','blk_..., dimensions={0} | all-to-all | bytes 1048576 | tf_op jit(solution)/shard_map/all_to_all | solution.py:514
  116.3 17.9 %all_to_all.31.gp = f32[128,8,128]{2,1,0:T(8,128)S(1)} all-to-all(f32[128,8,128]{2,1,0:T(8,128)S(1)} %summed.2), channel_id=1, replica_groups=mesh['wide_0'=4,'wide_1'=2,'blk_0'=4,'blk_1'=4] {'wide_0','wide_1','blk_..., dimensions={0} | all-to-all | bytes 1048576 | tf_op jit(solution)/shard_map/all_to_all | solution.py:514
  134.2 5.4 %all-to-all-start.3 = ((bf16[128,64,256]{2,1,0:T(8,128)(2,1)}), bf16[128,64,256]{2,1,0:T(8,128)(2,1)}, u32[]{:S(2)}, u32[]{:S(2)}) async-start(bf16[128,64,256]{2,1,0:T(8,128)(2,1)} %get-tuple-element.31), calls=%async_computation.3 | async-start | bytes 8388608 | tf_op jit(solution)/shard_map/all_to_all | solution.py:514
  139.6 1.4 collective-permute-start.2
  141.1 3.8 %collective-permute-start.3 = (f32[256,256]{1,0:T(8,128)S(1)}, f32[256,256]{1,0:T(8,128)S(1)}, u32[]{:S(2)}, u32[]{:S(2)}) collective-permute-start(f32[256,256]{1,0:T(8,128)S(1)} %copy-done.9), channel_id=1, source_target_pairs={{1,0},{2,1},{3,2},{4,3},{5,4},{6,5},{7,6},{8,7},{9,8},{10,9},{11,1... | collective-permute-start | bytes 786440 | tf_op jit(solution)/shard_map/ppermute | solution.py:521
  144.9 9.8 %solve.2 = (f32[256,256]{1,0:T(8,128)}, bf16[256,256]{1,0:T(8,128)(2,1)S(1)}, bf16[256,256]{1,0:T(8,128)(2,1)S(1)}) custom-call(f32[128,8,128]{2,1,0:T(8,128)S(1)} %all_to_all.31.gp), custom_call_target="tpu_custom_call" | custom-call | flops 12000000000 | bytes 1000000 | tf_op jit(solution)/shard_map/solve/pallas_call | solution.py:369
  156.0 18.1 %near1.1 = (f32[4096,256]{1,0:T(8,128)}, f32[4096,256]{1,0:T(8,128)}, f32[4096,256]{1,0:T(8,128)}) custom-call(f32[4096,256]{1,0:T(8,128)} %r.7, f32[4096,256]{1,0:T(8,128)} %get-tuple-element.23.image, bf16[256,256]{1,0:T(8,128)(2,1)} %copy-done, bf16[256,256]{1,0:T(8,128)(2,1)} %copy-done.1, bf16[4096,1536]{1,0:T(8,128)(2,1)} %right.3), custom_call_target="tpu_custom_call" | custom-call | flops 8000000000 | bytes 36000000 | tf_op jit(solution)/shard_map/near1/pallas_call | solution.py:407
  174.2 20.5 %collective-permute-done.2.ilo = f32[256,256]{1,0:T(8,128)S(1)} collective-permute-done((f32[256,256]{1,0:T(8,128)S(1)}, f32[256,256]{1,0:T(8,128)S(1)}, u32[]{:S(2)}, u32[]{:S(2)}) %collective-permute-start.2) | collective-permute-done | bytes 262176 | tf_op jit(solution)/shard_map/ppermute | solution.py:521
  195.5 19.5 %far1.1 = (f32[4096,256]{1,0:T(8,128)}, f32[128,8,128]{2,1,0:T(8,128)}) custom-call(s32[128]{0:T(128)} %bitcast.11, bf16[128,64,256]{2,1,0:T(8,128)(2,1)} %all-to-all-done.3.incoming, bf16[2048,256]{1,0:T(8,128)(2,1)} %reshape.15.coup, bf16[4096,64]{1,0:T(8,128)(2,1)} %copy.10.tb, f32[4096,256]{1,0:T(8,128)} %get-tuple-element.32.base, ...), custom_call_target="tpu_custom_call" | custom-call | tf_op jit(solution)/shard_map/far1/pallas_call | solution.py:464
  215.0 20.5 %all_to_all.32.parts = f32[128,8,128]{2,1,0:T(8,128)S(1)} all-to-all(f32[128,8,128]{2,1,0:T(8,128)} %get-tuple-element.37), channel_id=1, replica_groups=mesh['wide_0'=4,'wide_1'=2,'blk_0'=4,'blk_1'=4] {'wide_0','wide_1','blk_..., dimensions={0} | all-to-all | bytes 1048576 | tf_op jit(solution)/shard_map/all_to_all | solution.py:514
  235.6 17.9 %all_to_all.33.gp = f32[128,8,128]{2,1,0:T(8,128)S(1)} all-to-all(f32[128,8,128]{2,1,0:T(8,128)S(1)} %summed.3), channel_id=1, replica_groups=mesh['wide_0'=4,'wide_1'=2,'blk_0'=4,'blk_1'=4] {'wide_0','wide_1','blk_..., dimensions={0} | all-to-all | bytes 1048576 | tf_op jit(solution)/shard_map/all_to_all | solution.py:514
  253.5 9.8 %solve.3 = (f32[256,256]{1,0:T(8,128)}, bf16[256,256]{1,0:T(8,128)(2,1)S(1)}, bf16[256,256]{1,0:T(8,128)(2,1)S(1)}) custom-call(f32[128,8,128]{2,1,0:T(8,128)S(1)} %all_to_all.33.gp), custom_call_target="tpu_custom_call" | custom-call | flops 12000000000 | bytes 1000000 | tf_op jit(solution)/shard_map/solve/pallas_call | solution.py:369
  264.6 11.8 %finish.1 = (f32[4096,256]{1,0:T(8,128)}, f32[4096,256]{1,0:T(8,128)}) custom-call(f32[4096,256]{1,0:T(8,128)} %get-tuple-element.29.sol, f32[4096,256]{1,0:T(8,128)} %get-tuple-element.30.r, f32[4096,256]{1,0:T(8,128)} %get-tuple-element.36.image, bf16[256,256]{1,0:T(8,128)(2,1)} %copy-done.2, bf16[256,256]{1,0:T(8,128)(2,1)} %copy-done.3), custom_call_target="tpu_custom_call" | custom-call | tf_op jit(solution)/shard_map/finish/pallas_call | solution.py:502
  (28 shorter events, 4.5 us)
Async XLA Ops:
  7.9 66.9 %all-to-all-start = ((bf16[128,64,256]{2,1,0:T(8,128)(2,1)}), bf16[128,64,256]{2,1,0:T(8,128)(2,1)}, u32[]{:S(2)}, u32[]{:S(2)}) async-start(bf16[128,64,256]{2,1,0:T(8,128)(2,1)} %front.1), calls=%async_computation | async-start | bytes 8388608 | tf_op jit(solution)/shard_map/all_to_all | solution.py:514
  19.8 12.3 %copy-start.6 = (bf16[4096,64]{0,1:T(8,128)(2,1)S(1)}, bf16[4096,64]{0,1:T(8,128)(2,1)}, u32[]{:S(2)}) copy-start(bf16[4096,64]{0,1:T(8,128)(2,1)} %param.10) | copy-start | bytes 1572868
  21.7 53.0 %collective-permute-start = (f32[256,256]{1,0:T(8,128)}, f32[256,256]{1,0:T(8,128)S(1)}, u32[]{:S(2)}, u32[]{:S(2)}) collective-permute-start(f32[256,256]{1,0:T(8,128)} %get-tuple-element.41), channel_id=1, source_target_pairs={{0,1},{1,2},{2,3},{3,4},{4,5},{5,6},{6,7},{7,8},{8,9},{9,10},{10,1... | collective-permute-start | bytes 786440 | tf_op jit(solution)/shard_map/ppermute | solution.py:521
  23.0 51.7 %collective-permute-start.1 = (f32[256,256]{1,0:T(8,128)S(1)}, f32[256,256]{1,0:T(8,128)S(1)}, u32[]{:S(2)}, u32[]{:S(2)}) collective-permute-start(f32[256,256]{1,0:T(8,128)S(1)} %get-tuple-element.40), channel_id=1, source_target_pairs={{1,0},{2,1},{3,2},{4,3},{5,4},{6,5},{7,6},{8,7},{9,8},{10,9},{11,1... | collective-permute-start | bytes 786440 | tf_op jit(solution)/shard_map/ppermute | solution.py:521
  74.7 0.7 copy-start.4
  74.7 0.8 copy-start.5
  134.2 5.4 %copy-start.10 = (f32[256,256]{1,0:T(8,128)S(1)}, f32[256,256]{1,0:T(8,128)}, u32[]{:S(2)}) copy-start(f32[256,256]{1,0:T(8,128)} %get-tuple-element.34) | copy-start | bytes 786436
  134.2 6.9 %copy-start.9 = (f32[256,256]{1,0:T(8,128)S(1)}, f32[256,256]{1,0:T(8,128)}, u32[]{:S(2)}) copy-start(f32[256,256]{1,0:T(8,128)} %get-tuple-element.35) | copy-start | bytes 786436
  134.2 60.5 %all-to-all-start.3 = ((bf16[128,64,256]{2,1,0:T(8,128)(2,1)}), bf16[128,64,256]{2,1,0:T(8,128)(2,1)}, u32[]{:S(2)}, u32[]{:S(2)}) async-start(bf16[128,64,256]{2,1,0:T(8,128)(2,1)} %get-tuple-element.31), calls=%async_computation.3 | async-start | bytes 8388608 | tf_op jit(solution)/shard_map/all_to_all | solution.py:514
  139.6 55.0 %collective-permute-start.2 = (f32[256,256]{1,0:T(8,128)S(1)}, f32[256,256]{1,0:T(8,128)S(1)}, u32[]{:S(2)}, u32[]{:S(2)}) collective-permute-start(f32[256,256]{1,0:T(8,128)S(1)} %copy-done.10), channel_id=1, source_target_pairs={{0,1},{1,2},{2,3},{3,4},{4,5},{5,6},{6,7},{7,8},{8,9},{9,10},{10,1... | collective-permute-start | bytes 786440 | tf_op jit(solution)/shard_map/ppermute | solution.py:521
  141.1 53.6 %collective-permute-start.3 = (f32[256,256]{1,0:T(8,128)S(1)}, f32[256,256]{1,0:T(8,128)S(1)}, u32[]{:S(2)}, u32[]{:S(2)}) collective-permute-start(f32[256,256]{1,0:T(8,128)S(1)} %copy-done.9), channel_id=1, source_target_pairs={{1,0},{2,1},{3,2},{4,3},{5,4},{6,5},{7,6},{8,7},{9,8},{10,9},{11,1... | collective-permute-start | bytes 786440 | tf_op jit(solution)/shard_map/ppermute | solution.py:521
  154.7 0.7 copy-start
  155.4 0.7 copy-start.1
  194.7 0.7 copy-start.7
  194.7 0.8 copy-start.8
  263.3 0.6 copy-start.2
  264.0 0.6 copy-start.3

commit v3 on v2

--- a/solution.py
+++ b/solution.py
@@ -27,6 +27,10 @@
 
 
 def whole(*shape):
+    return pl.BlockSpec(shape, lambda t: (0,) * len(shape), pipeline_mode=pl.Buffered(1))
+
+
+def kept(*shape):
     return pl.BlockSpec(shape, lambda t: (0,) * len(shape))
 
 
@@ -94,7 +98,7 @@
         grid=(rows // TILE,),
         in_specs=[smem(), tiled(TILE, WIDTH), across(RANK, TILE)],
         out_specs=hbm(),
-        out_shape=jax.ShapeDtypeStruct((count, RANK, WIDTH), BF16),
+        out_shape=pltpu.HBM((count, RANK, WIDTH), BF16),
         scratch_shapes=[
             pltpu.VMEM((rows // LEAF, RANK, WIDTH), BF16),
             pltpu.SemaphoreType.DMA(()),
@@ -156,20 +160,16 @@
     def _():
         acc[...] = jnp.zeros(acc.shape, F32)
 
-    turned = ih.T
-    left = jnp.concatenate([turned, turned, il.T], axis=1)
-    gram = jnp.concatenate([ih, il, ih], axis=0)
-    proj = jnp.concatenate([rh, rl, rh], axis=0)
-    acc[...] += dot(left, jnp.concatenate([gram, proj], axis=1))
+    high = jnp.concatenate([ih.T, rh.T], axis=0)
+    low = jnp.concatenate([il.T, rl.T], axis=0)
+    acc[...] += dot(jnp.concatenate([high, high, low], axis=1), jnp.concatenate([ih, il, ih], axis=0))
     return ih, il
 
 
 def gram_end(acc, out):
-    for i in range(WIDTH // 8):
-        cut = slice(8 * i, 8 * i + 8)
+    for i in range(2 * WIDTH // 8):
         for h in range(2):
-            out[2 * i + h] = acc[cut, 128 * h : 128 * h + 128]
-            out[64 + 2 * i + h] = acc[cut, WIDTH + 128 * h : WIDTH + 128 * h + 128]
+            out[2 * i + h] = acc[8 * i : 8 * i + 8, 128 * h : 128 * h + 128]
 
 
 def slots_of(readers, incoming, leaf):
@@ -182,7 +182,7 @@
         whole(HALO, WIDTH),
         whole(HALO, WIDTH),
         pl.BlockSpec((TILE, HALO), lambda t: (jnp.minimum(t, edge - 1), 0)),
-        pl.BlockSpec((TILE, HALO), lambda t: (jnp.maximum(t, tiles - edge), (NEAR + HALO) // HALO)),
+        pl.BlockSpec((TILE, HALO), lambda t: (jnp.maximum(t - (tiles - edge), 0), 0)),
     ]
 
 
@@ -226,7 +226,7 @@
     @pl.when(t == pl.num_programs(0) - 1)
     def _():
         gram_end(acc, gp)
-        gram, total = acc[:, :WIDTH], acc[:, WIDTH:]
+        gram, total = acc[:WIDTH], acc[WIDTH:]
         eye = lax.broadcasted_iota(jnp.int32, gram.shape, 0) == lax.broadcasted_iota(jnp.int32, gram.shape, 1)
         g = jnp.sum(jnp.where(eye, gram, 0.0), axis=0, keepdims=True)
         p = jnp.sum(jnp.where(eye, total, 0.0), axis=0, keepdims=True)
@@ -237,7 +237,7 @@
         send_rows(packed, ids, out, sem, out.shape[0])
 
 
-def far0(ids, readers, incoming, coup, tb, s, base, r, err, lo, hi, near):
+def far0(ids, readers, incoming, coup, tb, s, base, r, err, lo, hi, left, right):
     rows = r.shape[0]
     leaves = rows // LEAF
     count = ids.shape[0]
@@ -259,10 +259,10 @@
         ],
         out_specs=[
             tiled(TILE, WIDTH),
-            whole(HALO, WIDTH),
-            whole(HALO, WIDTH),
+            kept(HALO, WIDTH),
+            kept(HALO, WIDTH),
             tiled(per * RANK, WIDTH),
-            whole(128, 8, 128),
+            kept(128, 8, 128),
             hbm(),
         ],
         out_shape=[
@@ -271,17 +271,17 @@
             jax.ShapeDtypeStruct((HALO, WIDTH), F32),
             jax.ShapeDtypeStruct((leaves * RANK, WIDTH), F32),
             jax.ShapeDtypeStruct((128, 8, 128), F32),
-            jax.ShapeDtypeStruct((count, RANK, WIDTH), BF16),
+            pltpu.HBM((count, RANK, WIDTH), BF16),
         ],
         scratch_shapes=[
             pltpu.VMEM((leaves, RANK, WIDTH), BF16),
             pltpu.VMEM((leaves, RANK, WIDTH), F32),
-            pltpu.VMEM((WIDTH, 2 * WIDTH), F32),
+            pltpu.VMEM((2 * WIDTH, WIDTH), F32),
             pltpu.SemaphoreType.DMA(()),
         ],
         compiler_params=params(FULL),
         name="far0",
-    )(ids, readers, incoming, coup, tb, s, base, r, err, lo, hi, near, near)
+    )(ids, readers, incoming, coup, tb, s, base, r, err, lo, hi, left, right)
 
 
 def sum_kernel(parts, out):
@@ -350,8 +350,8 @@
     a12 = block(0, 0, 16, 1)
     a21 = block(0, 16, 32, 0)
     w = exact(x11, a12)
-    b1 = jnp.concatenate([block(64, 0, 16, 0), block(64, 0, 16, 1)], axis=1)
-    b2 = jnp.concatenate([block(64, 16, 32, 0), block(64, 16, 32, 1)], axis=1)
+    b1 = block(64, 0, 32, 0).T
+    b2 = block(64, 0, 32, 1).T
     schur = block(0, 16, 32, 1) - exact(a21, w)
     y1 = exact(x11, b1)
     z = b2 - exact(a21, y1)
@@ -457,7 +457,7 @@
         gram_end(acc, gp)
 
 
-def far1(readers, incoming, coup, tb, base, r, trans, ah, al, lo, hi, ilo, ihi, near):
+def far1(readers, incoming, coup, tb, base, r, trans, ah, al, lo, hi, ilo, ihi, left, right):
     rows = r.shape[0]
     count = incoming.shape[0]
     per = TILE // LEAF
@@ -478,17 +478,17 @@
             whole(HALO, WIDTH),
             *edge_specs(rows // TILE),
         ],
-        out_specs=[tiled(TILE, WIDTH), whole(128, 8, 128)],
+        out_specs=[tiled(TILE, WIDTH), kept(128, 8, 128)],
         out_shape=[
             jax.ShapeDtypeStruct((rows, WIDTH), F32),
             jax.ShapeDtypeStruct((128, 8, 128), F32),
         ],
         scratch_shapes=[
-            pltpu.VMEM((WIDTH, 2 * WIDTH), F32),
+            pltpu.VMEM((2 * WIDTH, WIDTH), F32),
         ],
         compiler_params=params(FULL),
         name="far1",
-    )(readers, incoming, coup, tb, base, r, trans, ah, al, lo, hi, ilo, ihi, near, near)
+    )(readers, incoming, coup, tb, base, r, trans, ah, al, lo, hi, ilo, ihi, left, right)
 
 
 def finish_kernel(sol, r, image, ah, al, solution, residual):
@@ -505,7 +505,7 @@
         in_specs=[tiled(TILE, WIDTH)] * 3 + [whole(WIDTH, WIDTH)] * 2,
         out_specs=[tiled(TILE, WIDTH)] * 2,
         out_shape=[jax.ShapeDtypeStruct((rows, WIDTH), F32)] * 2,
-        compiler_params=params(FULL),
+        compiler_params=params(8),
         name="finish",
     )(sol, r, image, ah, al)
 
@@ -528,10 +528,12 @@
     source = source_basis.T
     incoming = exchange(front(ids, rhs, source))
     coup = far_coupling.transpose(0, 2, 1, 3).reshape(leaves * RANK, 4 * RANK)
+    left = near_blocks[:NEAR, :HALO]
+    right = near_blocks[-NEAR:, -HALO:]
     lo, hi = sides(rhs[:HALO], rhs[-HALO:])
     base0, err = near0(rhs, near_blocks, source)
     image0, first0, last0, trans0, gp0, outgoing = far0(
-        ids, readers, incoming, coup, target_basis, source, base0, rhs, err, lo, hi, near_blocks
+        ids, readers, incoming, coup, target_basis, source, base0, rhs, err, lo, hi, left, right
     )
     total = summed(exchange(gp0))
     total, outgoing = lax.optimization_barrier((total, outgoing))
@@ -541,7 +543,7 @@
     _, ah, al = solve(whole0)
     r1, base1, sol = near1(rhs, image0, ah, al, near_blocks)
     image1, gp1 = far1(
-        readers, incoming1, coup, target_basis, base1, r1, trans0, ah, al, lo, hi, ilo, ihi, near_blocks
+        readers, incoming1, coup, target_basis, base1, r1, trans0, ah, al, lo, hi, ilo, ihi, left, right
     )
     whole1 = exchange(summed(exchange(gp1)))
     _, bh, bl = solve(whole1)

time: 278 us -> 271 us (0.975)
  Pallas kernels: 110 us -> 105 us
    pallas_call x1, Pallas kernels: 11.8 us -> 6.7 us  [finish(): pl.pallas_call(finish_kernel, grid=(rows // TILE,), in_specs=[tiled(TILE,...]
  transfers between devices with their start and end apart: 6 -> 6, of which waited for: 2 -> 2; matrix products, arithmetic and copies ran while one was open for 3% -> 4% of each run, Pallas kernels for 15% -> 15%
where the time goes in v3:
time: 271 us; the launch traced here: 270 us
  Pallas kernels  105 us (39%)
  blocking collectives  76.6 us (28%)
  waiting for transfers between devices  46.8 us (17%)
  starting transfers between devices  27.4 us (10%)
  local copies, waits for them, and re-layouts  14 us (5%)
    all_to_all x4, blocking collectives, exchange(): lax.all_to_all(value, WIDE_BLK, split_axis=0, concat_axis=0, tiled=True)  76.6 us
    ppermute x4, waiting for transfers between devices, sides(): return (lax.ppermute(last, BLK, up), lax.ppermute(first, BLK, down))  46.7 us
    pallas_call x1, Pallas kernels, far0(): pl.pallas_call(far0_kernel, grid=(rows // TILE,), in_specs=[smem(), smem(...  20.3 us
    pallas_call x1, Pallas kernels, far1(): pl.pallas_call(far1_kernel, grid=(rows // TILE,), in_specs=[smem(), whole...  19.8 us
    pallas_call x2, Pallas kernels, solve(): pl.pallas_call(solve_kernel, out_shape=[jax.ShapeDtypeStruct((WIDTH, WIDT...  19.7 us
    pallas_call x1, Pallas kernels, near1(): pl.pallas_call(near1_kernel, grid=(rows // TILE,), in_specs=[whole(rows,...  18.1 us
    all_to_all x2, starting transfers between devices, exchange(): lax.all_to_all(value, WIDE_BLK, split_axis=0, concat_axis=0, tiled=True)  17.4 us
    pallas_call x1, Pallas kernels, near0(): pl.pallas_call(near0_kernel, grid=(rows // TILE,), in_specs=[whole(rows,...  12.8 us
  transfers between devices with their start and end apart: 6, of which 2 were waited for; matrix products, arithmetic and copies ran while one was open for 4% of the time, Pallas kernels for 15%

profile of v3, /device:TPU:1, one launch (start us, length us, event | category | flops | bytes accessed | tf_op | source)
XLA Modules:
  0.0 270.4 jit_solution(236740673334448457)
XLA Ops:
  0.6 7.2 %front.1 = bf16[128,64,256]{2,1,0:T(8,128)(2,1)} custom-call(s32[128]{0:T(128)} %bitcast.8, f32[4096,256]{1,0:T(8,128)} %r.7, bf16[64,4096]{1,0:T(8,128)(2,1)} %bitcast.4), custom_call_target="tpu_custom_call" | custom-call | tf_op jit(solution)/shard_map/front/pallas_call | solution.py:96
  7.9 12.0 %all-to-all-start = ((bf16[128,64,256]{2,1,0:T(8,128)(2,1)}), bf16[128,64,256]{2,1,0:T(8,128)(2,1)}, u32[]{:S(2)}, u32[]{:S(2)}) async-start(bf16[128,64,256]{2,1,0:T(8,128)(2,1)} %front.1), calls=%async_computation | async-start | bytes 8388608 | tf_op jit(solution)/shard_map/all_to_all | solution.py:514
  19.8 1.8 fusion.1
  21.7 1.4 collective-permute-start
  23.0 3.4 %collective-permute-start.1 = (f32[256,256]{1,0:T(8,128)S(1)}, f32[256,256]{1,0:T(8,128)S(1)}, u32[]{:S(2)}, u32[]{:S(2)}) collective-permute-start(f32[256,256]{1,0:T(8,128)S(1)} %get-tuple-element.42), channel_id=1, source_target_pairs={{1,0},{2,1},{3,2},{4,3},{5,4},{6,5},{7,6},{8,7},{9,8},{10,9},{11,1... | collective-permute-start | bytes 786440 | tf_op jit(solution)/shard_map/ppermute | solution.py:521
  26.5 3.6 %copy.9 = bf16[32,64,4,64]{3,2,1,0:T(4,128)(2,1)S(1)} copy(bf16[32,64,4,64]{3,1,2,0:T(8,128)(2,1)} %bitcast.7) | data formatting | bytes 2097152 | tf_op jit(solution)/shard_map/transpose | solution.py:530
  30.0 2.2 reshape.15.coup
  33.5 12.8 %near0.1 = (f32[4096,256]{1,0:T(8,128)}, f32[32,64,256]{2,1,0:T(8,128)}) custom-call(f32[4096,256]{1,0:T(8,128)} %r.7, bf16[4096,1536]{1,0:T(8,128)(2,1)} %near.3, bf16[64,4096]{1,0:T(8,128)(2,1)} %bitcast.5), custom_call_target="tpu_custom_call" | custom-call | flops 4000000000 | bytes 24000000 | tf_op jit(solution)/shard_map/near0/pallas_call | solution.py:135
  46.2 2.3 fusion
  48.5 26.2 %collective-permute-done.lo = f32[256,256]{1,0:T(8,128)S(1)} collective-permute-done((f32[256,256]{1,0:T(8,128)}, f32[256,256]{1,0:T(8,128)S(1)}, u32[]{:S(2)}, u32[]{:S(2)}) %collective-permute-start) | collective-permute-done | bytes 262176 | tf_op jit(solution)/shard_map/ppermute | solution.py:521
  75.5 20.3 %far0.1 = (f32[4096,256]{1,0:T(8,128)}, f32[256,256]{1,0:T(8,128)}, f32[256,256]{1,0:T(8,128)}, f32[2048,256]{1,0:T(8,128)}, f32[128,8,128]{2,1,0:T(8,128)}, /*index=5*/bf16[128,64,256]{2,1,0:T(8,128)(2,1)}) custom-call(s32[128]{0:T(128)} %bitcast.9, s32[128]{0:T(128)} %bitcast.10, bf16[128,64,256]{2,1,0:T(8,128)(2,1)} %all-to-all-done.incoming, ...), custom_call_target="tpu_custom_call" | custom-call | tf_op jit(solution)/shard_map/far0/pallas_call | solution.py:245
  95.8 20.4 %all_to_all.30.parts = f32[128,8,128]{2,1,0:T(8,128)S(1)} all-to-all(f32[128,8,128]{2,1,0:T(8,128)} %get-tuple-element.24), channel_id=1, replica_groups=mesh['wide_0'=4,'wide_1'=2,'blk_0'=4,'blk_1'=4] {'wide_0','wide_1','blk_..., dimensions={0} | all-to-all | bytes 1048576 | tf_op jit(solution)/shard_map/all_to_all | solution.py:514
  116.4 17.9 %all_to_all.31.gp = f32[128,8,128]{2,1,0:T(8,128)S(1)} all-to-all(f32[128,8,128]{2,1,0:T(8,128)S(1)} %summed.2), channel_id=1, replica_groups=mesh['wide_0'=4,'wide_1'=2,'blk_0'=4,'blk_1'=4] {'wide_0','wide_1','blk_..., dimensions={0} | all-to-all | bytes 1048576 | tf_op jit(solution)/shard_map/all_to_all | solution.py:514
  134.3 5.4 %all-to-all-start.3 = ((bf16[128,64,256]{2,1,0:T(8,128)(2,1)}), bf16[128,64,256]{2,1,0:T(8,128)(2,1)}, u32[]{:S(2)}, u32[]{:S(2)}) async-start(bf16[128,64,256]{2,1,0:T(8,128)(2,1)} %get-tuple-element.31), calls=%async_computation.3 | async-start | bytes 8388608 | tf_op jit(solution)/shard_map/all_to_all | solution.py:514
  139.8 1.4 collective-permute-start.2
  141.2 3.8 %collective-permute-start.3 = (f32[256,256]{1,0:T(8,128)S(1)}, f32[256,256]{1,0:T(8,128)S(1)}, u32[]{:S(2)}, u32[]{:S(2)}) collective-permute-start(f32[256,256]{1,0:T(8,128)S(1)} %copy-done.10), channel_id=1, source_target_pairs={{1,0},{2,1},{3,2},{4,3},{5,4},{6,5},{7,6},{8,7},{9,8},{10,9},{11,1... | collective-permute-start | bytes 786440 | tf_op jit(solution)/shard_map/ppermute | solution.py:521
  145.0 9.8 %solve.2 = (f32[256,256]{1,0:T(8,128)}, bf16[256,256]{1,0:T(8,128)(2,1)S(1)}, bf16[256,256]{1,0:T(8,128)(2,1)S(1)}) custom-call(f32[128,8,128]{2,1,0:T(8,128)S(1)} %all_to_all.31.gp), custom_call_target="tpu_custom_call" | custom-call | flops 12000000000 | bytes 1000000 | tf_op jit(solution)/shard_map/solve/pallas_call | solution.py:369
  156.2 18.1 %near1.1 = (f32[4096,256]{1,0:T(8,128)}, f32[4096,256]{1,0:T(8,128)}, f32[4096,256]{1,0:T(8,128)}) custom-call(f32[4096,256]{1,0:T(8,128)} %r.7, f32[4096,256]{1,0:T(8,128)} %get-tuple-element.23.image, bf16[256,256]{1,0:T(8,128)(2,1)} %copy-done.3, bf16[256,256]{1,0:T(8,128)(2,1)} %copy-done.4, bf16[4096,1536]{1,0:T(8,128)(2,1)} %near.3), custom_call_target="tpu_custom_call" | custom-call | flops 8000000000 | bytes 36000000 | tf_op jit(solution)/shard_map/near1/pallas_call | solution.py:407
  174.3 20.5 %collective-permute-done.2.ilo = f32[256,256]{1,0:T(8,128)S(1)} collective-permute-done((f32[256,256]{1,0:T(8,128)S(1)}, f32[256,256]{1,0:T(8,128)S(1)}, u32[]{:S(2)}, u32[]{:S(2)}) %collective-permute-start.2) | collective-permute-done | bytes 262176 | tf_op jit(solution)/shard_map/ppermute | solution.py:521
  195.6 19.8 %far1.1 = (f32[4096,256]{1,0:T(8,128)}, f32[128,8,128]{2,1,0:T(8,128)}) custom-call(s32[128]{0:T(128)} %bitcast.11, bf16[128,64,256]{2,1,0:T(8,128)(2,1)} %all-to-all-done.3.incoming, bf16[2048,256]{1,0:T(8,128)(2,1)} %reshape.15.coup, bf16[4096,64]{1,0:T(8,128)(2,1)} %copy.10.tb, f32[4096,256]{1,0:T(8,128)} %get-tuple-element.32.base, ...), custom_call_target="tpu_custom_call" | custom-call | tf_op jit(solution)/shard_map/far1/pallas_call | solution.py:464
  215.4 20.4 %all_to_all.32.parts = f32[128,8,128]{2,1,0:T(8,128)S(1)} all-to-all(f32[128,8,128]{2,1,0:T(8,128)} %get-tuple-element.37), channel_id=1, replica_groups=mesh['wide_0'=4,'wide_1'=2,'blk_0'=4,'blk_1'=4] {'wide_0','wide_1','blk_..., dimensions={0} | all-to-all | bytes 1048576 | tf_op jit(solution)/shard_map/all_to_all | solution.py:514
  236.0 17.9 %all_to_all.33.gp = f32[128,8,128]{2,1,0:T(8,128)S(1)} all-to-all(f32[128,8,128]{2,1,0:T(8,128)S(1)} %summed.3), channel_id=1, replica_groups=mesh['wide_0'=4,'wide_1'=2,'blk_0'=4,'blk_1'=4] {'wide_0','wide_1','blk_..., dimensions={0} | all-to-all | bytes 1048576 | tf_op jit(solution)/shard_map/all_to_all | solution.py:514
  253.9 9.8 %solve.3 = (f32[256,256]{1,0:T(8,128)}, bf16[256,256]{1,0:T(8,128)(2,1)S(1)}, bf16[256,256]{1,0:T(8,128)(2,1)S(1)}) custom-call(f32[128,8,128]{2,1,0:T(8,128)S(1)} %all_to_all.33.gp), custom_call_target="tpu_custom_call" | custom-call | flops 12000000000 | bytes 1000000 | tf_op jit(solution)/shard_map/solve/pallas_call | solution.py:369
  263.7 6.7 %finish.1 = (f32[4096,256]{1,0:T(8,128)}, f32[4096,256]{1,0:T(8,128)}) custom-call(f32[4096,256]{1,0:T(8,128)S(1)} %copy-done.1, f32[4096,256]{1,0:T(8,128)S(1)} %copy-done, f32[4096,256]{1,0:T(8,128)S(1)} %copy-done.2, bf16[256,256]{1,0:T(8,128)(2,1)S(1)} %get-tuple-element.38.ah, bf16[256,256]{1,0:T(8,128)(2,1)S(1)} %get-tuple-element.39.al), custom_call_target="tpu_custom_call" | custom-call | tf_op jit(solution)/shard_map/finish/pallas_call | solution.py:502
  (31 shorter events, 4.6 us)
Async XLA Ops:
  7.9 66.9 %all-to-all-start = ((bf16[128,64,256]{2,1,0:T(8,128)(2,1)}), bf16[128,64,256]{2,1,0:T(8,128)(2,1)}, u32[]{:S(2)}, u32[]{:S(2)}) async-start(bf16[128,64,256]{2,1,0:T(8,128)(2,1)} %front.1), calls=%async_computation | async-start | bytes 8388608 | tf_op jit(solution)/shard_map/all_to_all | solution.py:514
  19.8 12.3 %copy-start.7 = (bf16[4096,64]{0,1:T(8,128)(2,1)S(1)}, bf16[4096,64]{0,1:T(8,128)(2,1)}, u32[]{:S(2)}) copy-start(bf16[4096,64]{0,1:T(8,128)(2,1)} %param.10) | copy-start | bytes 1572868
  21.7 53.1 %collective-permute-start = (f32[256,256]{1,0:T(8,128)}, f32[256,256]{1,0:T(8,128)S(1)}, u32[]{:S(2)}, u32[]{:S(2)}) collective-permute-start(f32[256,256]{1,0:T(8,128)} %get-tuple-element.43), channel_id=1, source_target_pairs={{0,1},{1,2},{2,3},{3,4},{4,5},{5,6},{6,7},{7,8},{8,9},{9,10},{10,1... | collective-permute-start | bytes 786440 | tf_op jit(solution)/shard_map/ppermute | solution.py:521
  23.0 51.7 %collective-permute-start.1 = (f32[256,256]{1,0:T(8,128)S(1)}, f32[256,256]{1,0:T(8,128)S(1)}, u32[]{:S(2)}, u32[]{:S(2)}) collective-permute-start(f32[256,256]{1,0:T(8,128)S(1)} %get-tuple-element.42), channel_id=1, source_target_pairs={{1,0},{2,1},{3,2},{4,3},{5,4},{6,5},{7,6},{8,7},{9,8},{10,9},{11,1... | collective-permute-start | bytes 786440 | tf_op jit(solution)/shard_map/ppermute | solution.py:521
  74.7 0.7 copy-start.5
  74.7 0.8 copy-start.6
  134.3 5.4 %copy-start.11 = (f32[256,256]{1,0:T(8,128)S(1)}, f32[256,256]{1,0:T(8,128)}, u32[]{:S(2)}) copy-start(f32[256,256]{1,0:T(8,128)} %get-tuple-element.34) | copy-start | bytes 786436
  134.3 6.9 %copy-start.10 = (f32[256,256]{1,0:T(8,128)S(1)}, f32[256,256]{1,0:T(8,128)}, u32[]{:S(2)}) copy-start(f32[256,256]{1,0:T(8,128)} %get-tuple-element.35) | copy-start | bytes 786436
  134.3 60.5 %all-to-all-start.3 = ((bf16[128,64,256]{2,1,0:T(8,128)(2,1)}), bf16[128,64,256]{2,1,0:T(8,128)(2,1)}, u32[]{:S(2)}, u32[]{:S(2)}) async-start(bf16[128,64,256]{2,1,0:T(8,128)(2,1)} %get-tuple-element.31), calls=%async_computation.3 | async-start | bytes 8388608 | tf_op jit(solution)/shard_map/all_to_all | solution.py:514
  139.8 55.0 %collective-permute-start.2 = (f32[256,256]{1,0:T(8,128)S(1)}, f32[256,256]{1,0:T(8,128)S(1)}, u32[]{:S(2)}, u32[]{:S(2)}) collective-permute-start(f32[256,256]{1,0:T(8,128)S(1)} %copy-done.11), channel_id=1, source_target_pairs={{0,1},{1,2},{2,3},{3,4},{4,5},{5,6},{6,7},{7,8},{8,9},{9,10},{10,1... | collective-permute-start | bytes 786440 | tf_op jit(solution)/shard_map/ppermute | solution.py:521
  141.2 53.6 %collective-permute-start.3 = (f32[256,256]{1,0:T(8,128)S(1)}, f32[256,256]{1,0:T(8,128)S(1)}, u32[]{:S(2)}, u32[]{:S(2)}) collective-permute-start(f32[256,256]{1,0:T(8,128)S(1)} %copy-done.10), channel_id=1, source_target_pairs={{1,0},{2,1},{3,2},{4,3},{5,4},{6,5},{7,6},{8,7},{9,8},{10,9},{11,1... | collective-permute-start | bytes 786440 | tf_op jit(solution)/shard_map/ppermute | solution.py:521
  154.9 0.6 copy-start.3
  155.5 0.7 copy-start.4
  194.8 0.7 copy-start.8
  194.8 0.8 copy-start.9
  253.8 9.8 %copy-start = (f32[4096,256]{1,0:T(8,128)S(1)}, f32[4096,256]{1,0:T(8,128)}, u32[]{:S(2)}) copy-start(f32[4096,256]{1,0:T(8,128)} %get-tuple-element.30.r) | copy-start | bytes 12582916
  253.8 9.8 %copy-start.1 = (f32[4096,256]{1,0:T(8,128)S(1)}, f32[4096,256]{1,0:T(8,128)}, u32[]{:S(2)}) copy-start(f32[4096,256]{1,0:T(8,128)} %get-tuple-element.29.sol) | copy-start | bytes 12582916
  253.8 9.8 %copy-start.2 = (f32[4096,256]{1,0:T(8,128)S(1)}, f32[4096,256]{1,0:T(8,128)}, u32[]{:S(2)}) copy-start(f32[4096,256]{1,0:T(8,128)} %get-tuple-element.36.image) | copy-start | bytes 12582916

commit v4 on v3

--- a/solution.py
+++ b/solution.py
@@ -12,7 +12,7 @@
 RANK = 64
 WIDTH = 256
 TILE = 512
-FULL = 58
+FULL = 56
 BLK = ("blk_0", "blk_1")
 WIDE_BLK = ("wide_0", "wide_1", "blk_0", "blk_1")
 F32 = jnp.float32
@@ -172,8 +172,28 @@
             out[2 * i + h] = acc[8 * i : 8 * i + 8, 128 * h : 128 * h + 128]
 
 
-def slots_of(readers, incoming, leaf):
-    return jnp.concatenate([incoming[readers[leaf * 4 + f]] for f in range(4)], axis=0)
+def fetch_slots(t, readers, incoming, slots, sems):
+    count = 4 * (TILE // LEAF)
+
+    def start(step):
+        for k in range(count):
+            pltpu.make_async_copy(
+                incoming.at[readers[step * count + k]],
+                slots.at[step % 2, pl.ds(k * RANK, RANK)],
+                sems.at[step % 2],
+            ).start()
+
+    @pl.when(t == 0)
+    def _():
+        start(t)
+
+    @pl.when(t + 1 < pl.num_programs(0))
+    def _():
+        start(t + 1)
+
+    now = slots.at[t % 2]
+    pltpu.make_async_copy(now, now, sems.at[t % 2]).wait()
+    return now
 
 
 def edge_specs(tiles):
@@ -198,13 +218,14 @@
         image[...] += dot(right[...], last())
 
 
-def far0_kernel(ids, readers, incoming, coup, tb, s, base, r, err, lo, hi, left, right, image, first, last, trans, gp, out, packed, direct, acc, sem):
+def far0_kernel(ids, readers, incoming, coup, tb, s, base, r, err, lo, hi, left, right, image, first, last, trans, gp, out, packed, direct, saved, acc, slots, sems, sem):
     t = pl.program_id(0)
     per = TILE // LEAF
+    now = fetch_slots(t, readers, incoming, slots, sems)
     tiles = []
     for i in range(per):
         cut = slice(i * LEAF, (i + 1) * LEAF)
-        tr = dot(coup[i * RANK : (i + 1) * RANK], slots_of(readers, incoming, t * per + i))
+        tr = dot(coup[i * RANK : (i + 1) * RANK], now[4 * i * RANK : 4 * (i + 1) * RANK])
         trans[i * RANK : (i + 1) * RANK] = tr
         tiles.append(base[cut] + dot(tb[cut], tr.astype(BF16)))
     image[...] = jnp.concatenate(tiles, axis=0)
@@ -222,6 +243,7 @@
     for i in range(per):
         cut = slice(i * LEAF, (i + 1) * LEAF)
         direct[t * per + i] = dot(s[:, cut], ih[cut]) + dot(s[:, cut], il[cut])
+        saved[t * per + i] = err[i]
 
     @pl.when(t == pl.num_programs(0) - 1)
     def _():
@@ -233,7 +255,7 @@
         fits = (4.0 * p > g) & (4.0 * g > p)
         guess = jnp.where(fits, g / jnp.where(fits, p, 1.0), 0.0)
         for leaf in range(packed.shape[0]):
-            packed[leaf] = (direct[leaf] + err[leaf] * guess).astype(BF16)
+            packed[leaf] = (direct[leaf] + saved[leaf] * guess).astype(BF16)
         send_rows(packed, ids, out, sem, out.shape[0])
 
 
@@ -248,13 +270,13 @@
         in_specs=[
             smem(),
             smem(),
-            whole(count, RANK, WIDTH),
+            hbm(),
             tiled(per * RANK, 4 * RANK),
             tiled(TILE, RANK),
             across(RANK, TILE),
             tiled(TILE, WIDTH),
             tiled(TILE, WIDTH),
-            whole(leaves, RANK, WIDTH),
+            tiled(per, RANK, WIDTH),
             *edge_specs(rows // TILE),
         ],
         out_specs=[
@@ -276,7 +298,10 @@
         scratch_shapes=[
             pltpu.VMEM((leaves, RANK, WIDTH), BF16),
             pltpu.VMEM((leaves, RANK, WIDTH), F32),
+            pltpu.VMEM((leaves, RANK, WIDTH), F32),
             pltpu.VMEM((2 * WIDTH, WIDTH), F32),
+            pltpu.VMEM((2, 4 * per * RANK, WIDTH), BF16),
+            pltpu.SemaphoreType.DMA((2,)),
             pltpu.SemaphoreType.DMA(()),
         ],
         compiler_params=params(FULL),
@@ -426,12 +451,13 @@
     )(r, image, ah, al, near)
 
 
-def far1_kernel(readers, incoming, coup, tb, base, r, trans, ah, al, lo, hi, ilo, ihi, left, right, image, gp, acc):
+def far1_kernel(readers, incoming, coup, tb, base, r, trans, ah, al, lo, hi, ilo, ihi, left, right, image, gp, acc, slots, sems):
     t = pl.program_id(0)
     per = TILE // LEAF
+    now = fetch_slots(t, readers, incoming, slots, sems)
     moved = jnp.concatenate(
         [
-            dot(coup[i * RANK : (i + 1) * RANK], slots_of(readers, incoming, t * per + i))
+            dot(coup[i * RANK : (i + 1) * RANK], now[4 * i * RANK : 4 * (i + 1) * RANK])
             for i in range(per)
         ],
         axis=0,
@@ -459,14 +485,13 @@
 
 def far1(readers, incoming, coup, tb, base, r, trans, ah, al, lo, hi, ilo, ihi, left, right):
     rows = r.shape[0]
-    count = incoming.shape[0]
     per = TILE // LEAF
     return pl.pallas_call(
         far1_kernel,
         grid=(rows // TILE,),
         in_specs=[
             smem(),
-            whole(count, RANK, WIDTH),
+            hbm(),
             tiled(per * RANK, 4 * RANK),
             tiled(TILE, RANK),
             tiled(TILE, WIDTH),
@@ -485,6 +510,8 @@
         ],
         scratch_shapes=[
             pltpu.VMEM((2 * WIDTH, WIDTH), F32),
+            pltpu.VMEM((2, 4 * per * RANK, WIDTH), BF16),
+            pltpu.SemaphoreType.DMA((2,)),
         ],
         compiler_params=params(FULL),
         name="far1",

time: 271 us -> 271 us (level)
  no operation moved by 1% of the time
where the time goes in v4:
time: 271 us; the launch traced here: 270 us
  Pallas kernels  105 us (39%)
  blocking collectives  76.6 us (28%)
  waiting for transfers between devices  46.8 us (17%)
  starting transfers between devices  27.4 us (10%)
  local copies, waits for them, and re-layouts  14 us (5%)
    all_to_all x4, blocking collectives, exchange(): lax.all_to_all(value, WIDE_BLK, split_axis=0, concat_axis=0, tiled=True)  76.6 us
    ppermute x4, waiting for transfers between devices, sides(): return (lax.ppermute(last, BLK, up), lax.ppermute(first, BLK, down))  46.7 us
    pallas_call x1, Pallas kernels, far1(): pl.pallas_call(far1_kernel, grid=(rows // TILE,), in_specs=[smem(), hbm()...  20 us
    pallas_call x1, Pallas kernels, far0(): pl.pallas_call(far0_kernel, grid=(rows // TILE,), in_specs=[smem(), smem(...  19.9 us
    pallas_call x2, Pallas kernels, solve(): pl.pallas_call(solve_kernel, out_shape=[jax.ShapeDtypeStruct((WIDTH, WIDT...  19.7 us
    pallas_call x1, Pallas kernels, near1(): pl.pallas_call(near1_kernel, grid=(rows // TILE,), in_specs=[whole(rows,...  18.1 us
    all_to_all x2, starting transfers between devices, exchange(): lax.all_to_all(value, WIDE_BLK, split_axis=0, concat_axis=0, tiled=True)  17.4 us
    pallas_call x1, Pallas kernels, near0(): pl.pallas_call(near0_kernel, grid=(rows // TILE,), in_specs=[whole(rows,...  12.8 us
  transfers between devices with their start and end apart: 6, of which 2 were waited for; matrix products, arithmetic and copies ran while one was open for 4% of the time, Pallas kernels for 15%

profile of v4, /device:TPU:1, one launch (start us, length us, event | category | flops | bytes accessed | tf_op | source)
XLA Modules:
  0.0 270.3 jit_solution(2895853448422580407)
XLA Ops:
  0.6 7.2 %front.1 = bf16[128,64,256]{2,1,0:T(8,128)(2,1)} custom-call(s32[128]{0:T(128)} %bitcast.8, f32[4096,256]{1,0:T(8,128)} %r.7, bf16[64,4096]{1,0:T(8,128)(2,1)} %bitcast.4), custom_call_target="tpu_custom_call" | custom-call | tf_op jit(solution)/shard_map/front/pallas_call | solution.py:96
  7.9 12.0 %all-to-all-start = ((bf16[128,64,256]{2,1,0:T(8,128)(2,1)}), bf16[128,64,256]{2,1,0:T(8,128)(2,1)}, u32[]{:S(2)}, u32[]{:S(2)}) async-start(bf16[128,64,256]{2,1,0:T(8,128)(2,1)} %front.1), calls=%async_computation | async-start | bytes 8388608 | tf_op jit(solution)/shard_map/all_to_all | solution.py:541
  19.8 1.8 fusion.1
  21.7 1.4 collective-permute-start
  23.0 3.4 %collective-permute-start.1 = (f32[256,256]{1,0:T(8,128)S(1)}, f32[256,256]{1,0:T(8,128)S(1)}, u32[]{:S(2)}, u32[]{:S(2)}) collective-permute-start(f32[256,256]{1,0:T(8,128)S(1)} %get-tuple-element.42), channel_id=1, source_target_pairs={{1,0},{2,1},{3,2},{4,3},{5,4},{6,5},{7,6},{8,7},{9,8},{10,9},{11,1... | collective-permute-start | bytes 786440 | tf_op jit(solution)/shard_map/ppermute | solution.py:548
  26.5 3.6 %copy.9 = bf16[32,64,4,64]{3,2,1,0:T(4,128)(2,1)S(1)} copy(bf16[32,64,4,64]{3,1,2,0:T(8,128)(2,1)} %bitcast.7) | data formatting | bytes 2097152 | tf_op jit(solution)/shard_map/transpose | solution.py:557
  30.0 2.2 reshape.15.coup
  33.5 12.8 %near0.1 = (f32[4096,256]{1,0:T(8,128)}, f32[32,64,256]{2,1,0:T(8,128)}) custom-call(f32[4096,256]{1,0:T(8,128)} %r.7, bf16[4096,1536]{1,0:T(8,128)(2,1)} %near.3, bf16[64,4096]{1,0:T(8,128)(2,1)} %bitcast.5), custom_call_target="tpu_custom_call" | custom-call | flops 4000000000 | bytes 24000000 | tf_op jit(solution)/shard_map/near0/pallas_call | solution.py:135
  46.2 2.3 fusion
  48.5 26.2 %collective-permute-done.lo = f32[256,256]{1,0:T(8,128)S(1)} collective-permute-done((f32[256,256]{1,0:T(8,128)}, f32[256,256]{1,0:T(8,128)S(1)}, u32[]{:S(2)}, u32[]{:S(2)}) %collective-permute-start) | collective-permute-done | bytes 262176 | tf_op jit(solution)/shard_map/ppermute | solution.py:548
  75.5 19.9 %far0.1 = (f32[4096,256]{1,0:T(8,128)}, f32[256,256]{1,0:T(8,128)}, f32[256,256]{1,0:T(8,128)}, f32[2048,256]{1,0:T(8,128)}, f32[128,8,128]{2,1,0:T(8,128)}, /*index=5*/bf16[128,64,256]{2,1,0:T(8,128)(2,1)}) custom-call(s32[128]{0:T(128)} %bitcast.9, s32[128]{0:T(128)} %bitcast.10, bf16[128,64,256]{2,1,0:T(8,128)(2,1)} %all-to-all-done.incoming, ...), custom_call_target="tpu_custom_call" | custom-call | tf_op jit(solution)/shard_map/far0/pallas_call | solution.py:267
  95.4 20.4 %all_to_all.30.parts = f32[128,8,128]{2,1,0:T(8,128)S(1)} all-to-all(f32[128,8,128]{2,1,0:T(8,128)} %get-tuple-element.24), channel_id=1, replica_groups=mesh['wide_0'=4,'wide_1'=2,'blk_0'=4,'blk_1'=4] {'wide_0','wide_1','blk_..., dimensions={0} | all-to-all | bytes 1048576 | tf_op jit(solution)/shard_map/all_to_all | solution.py:541
  116.0 17.9 %all_to_all.31.gp = f32[128,8,128]{2,1,0:T(8,128)S(1)} all-to-all(f32[128,8,128]{2,1,0:T(8,128)S(1)} %summed.2), channel_id=1, replica_groups=mesh['wide_0'=4,'wide_1'=2,'blk_0'=4,'blk_1'=4] {'wide_0','wide_1','blk_..., dimensions={0} | all-to-all | bytes 1048576 | tf_op jit(solution)/shard_map/all_to_all | solution.py:541
  133.9 5.4 %all-to-all-start.3 = ((bf16[128,64,256]{2,1,0:T(8,128)(2,1)}), bf16[128,64,256]{2,1,0:T(8,128)(2,1)}, u32[]{:S(2)}, u32[]{:S(2)}) async-start(bf16[128,64,256]{2,1,0:T(8,128)(2,1)} %get-tuple-element.31), calls=%async_computation.3 | async-start | bytes 8388608 | tf_op jit(solution)/shard_map/all_to_all | solution.py:541
  139.4 1.4 collective-permute-start.2
  140.8 3.8 %collective-permute-start.3 = (f32[256,256]{1,0:T(8,128)S(1)}, f32[256,256]{1,0:T(8,128)S(1)}, u32[]{:S(2)}, u32[]{:S(2)}) collective-permute-start(f32[256,256]{1,0:T(8,128)S(1)} %copy-done.10), channel_id=1, source_target_pairs={{1,0},{2,1},{3,2},{4,3},{5,4},{6,5},{7,6},{8,7},{9,8},{10,9},{11,1... | collective-permute-start | bytes 786440 | tf_op jit(solution)/shard_map/ppermute | solution.py:548
  144.6 9.8 %solve.2 = (f32[256,256]{1,0:T(8,128)}, bf16[256,256]{1,0:T(8,128)(2,1)S(1)}, bf16[256,256]{1,0:T(8,128)(2,1)S(1)}) custom-call(f32[128,8,128]{2,1,0:T(8,128)S(1)} %all_to_all.31.gp), custom_call_target="tpu_custom_call" | custom-call | flops 12000000000 | bytes 1000000 | tf_op jit(solution)/shard_map/solve/pallas_call | solution.py:394
  155.8 18.1 %near1.1 = (f32[4096,256]{1,0:T(8,128)}, f32[4096,256]{1,0:T(8,128)}, f32[4096,256]{1,0:T(8,128)}) custom-call(f32[4096,256]{1,0:T(8,128)} %r.7, f32[4096,256]{1,0:T(8,128)} %get-tuple-element.23.image, bf16[256,256]{1,0:T(8,128)(2,1)} %copy-done.3, bf16[256,256]{1,0:T(8,128)(2,1)} %copy-done.4, bf16[4096,1536]{1,0:T(8,128)(2,1)} %near.3), custom_call_target="tpu_custom_call" | custom-call | flops 8000000000 | bytes 36000000 | tf_op jit(solution)/shard_map/near1/pallas_call | solution.py:432
  173.9 20.5 %collective-permute-done.2.ilo = f32[256,256]{1,0:T(8,128)S(1)} collective-permute-done((f32[256,256]{1,0:T(8,128)S(1)}, f32[256,256]{1,0:T(8,128)S(1)}, u32[]{:S(2)}, u32[]{:S(2)}) %collective-permute-start.2) | collective-permute-done | bytes 262176 | tf_op jit(solution)/shard_map/ppermute | solution.py:548
  195.2 20.0 %far1.1 = (f32[4096,256]{1,0:T(8,128)}, f32[128,8,128]{2,1,0:T(8,128)}) custom-call(s32[128]{0:T(128)} %bitcast.11, bf16[128,64,256]{2,1,0:T(8,128)(2,1)} %all-to-all-done.3.incoming, bf16[2048,256]{1,0:T(8,128)(2,1)} %reshape.15.coup, bf16[4096,64]{1,0:T(8,128)(2,1)} %copy.10.tb, f32[4096,256]{1,0:T(8,128)} %get-tuple-element.32.base, ...), custom_call_target="tpu_custom_call" | custom-call | tf_op jit(solution)/shard_map/far1/pallas_call | solution.py:489
  215.2 20.4 %all_to_all.32.parts = f32[128,8,128]{2,1,0:T(8,128)S(1)} all-to-all(f32[128,8,128]{2,1,0:T(8,128)} %get-tuple-element.37), channel_id=1, replica_groups=mesh['wide_0'=4,'wide_1'=2,'blk_0'=4,'blk_1'=4] {'wide_0','wide_1','blk_..., dimensions={0} | all-to-all | bytes 1048576 | tf_op jit(solution)/shard_map/all_to_all | solution.py:541
  235.8 17.9 %all_to_all.33.gp = f32[128,8,128]{2,1,0:T(8,128)S(1)} all-to-all(f32[128,8,128]{2,1,0:T(8,128)S(1)} %summed.3), channel_id=1, replica_groups=mesh['wide_0'=4,'wide_1'=2,'blk_0'=4,'blk_1'=4] {'wide_0','wide_1','blk_..., dimensions={0} | all-to-all | bytes 1048576 | tf_op jit(solution)/shard_map/all_to_all | solution.py:541
  253.7 9.8 %solve.3 = (f32[256,256]{1,0:T(8,128)}, bf16[256,256]{1,0:T(8,128)(2,1)S(1)}, bf16[256,256]{1,0:T(8,128)(2,1)S(1)}) custom-call(f32[128,8,128]{2,1,0:T(8,128)S(1)} %all_to_all.33.gp), custom_call_target="tpu_custom_call" | custom-call | flops 12000000000 | bytes 1000000 | tf_op jit(solution)/shard_map/solve/pallas_call | solution.py:394
  263.6 6.7 %finish.1 = (f32[4096,256]{1,0:T(8,128)}, f32[4096,256]{1,0:T(8,128)}) custom-call(f32[4096,256]{1,0:T(8,128)S(1)} %copy-done.1, f32[4096,256]{1,0:T(8,128)S(1)} %copy-done, f32[4096,256]{1,0:T(8,128)S(1)} %copy-done.2, bf16[256,256]{1,0:T(8,128)(2,1)S(1)} %get-tuple-element.38.ah, bf16[256,256]{1,0:T(8,128)(2,1)S(1)} %get-tuple-element.39.al), custom_call_target="tpu_custom_call" | custom-call | tf_op jit(solution)/shard_map/finish/pallas_call | solution.py:529
  (31 shorter events, 4.6 us)
Async XLA Ops:
  7.9 66.9 %all-to-all-start = ((bf16[128,64,256]{2,1,0:T(8,128)(2,1)}), bf16[128,64,256]{2,1,0:T(8,128)(2,1)}, u32[]{:S(2)}, u32[]{:S(2)}) async-start(bf16[128,64,256]{2,1,0:T(8,128)(2,1)} %front.1), calls=%async_computation | async-start | bytes 8388608 | tf_op jit(solution)/shard_map/all_to_all | solution.py:541
  19.8 12.3 %copy-start.7 = (bf16[4096,64]{0,1:T(8,128)(2,1)S(1)}, bf16[4096,64]{0,1:T(8,128)(2,1)}, u32[]{:S(2)}) copy-start(bf16[4096,64]{0,1:T(8,128)(2,1)} %param.10) | copy-start | bytes 1572868
  21.7 53.1 %collective-permute-start = (f32[256,256]{1,0:T(8,128)}, f32[256,256]{1,0:T(8,128)S(1)}, u32[]{:S(2)}, u32[]{:S(2)}) collective-permute-start(f32[256,256]{1,0:T(8,128)} %get-tuple-element.43), channel_id=1, source_target_pairs={{0,1},{1,2},{2,3},{3,4},{4,5},{5,6},{6,7},{7,8},{8,9},{9,10},{10,1... | collective-permute-start | bytes 786440 | tf_op jit(solution)/shard_map/ppermute | solution.py:548
  23.0 51.7 %collective-permute-start.1 = (f32[256,256]{1,0:T(8,128)S(1)}, f32[256,256]{1,0:T(8,128)S(1)}, u32[]{:S(2)}, u32[]{:S(2)}) collective-permute-start(f32[256,256]{1,0:T(8,128)S(1)} %get-tuple-element.42), channel_id=1, source_target_pairs={{1,0},{2,1},{3,2},{4,3},{5,4},{6,5},{7,6},{8,7},{9,8},{10,9},{11,1... | collective-permute-start | bytes 786440 | tf_op jit(solution)/shard_map/ppermute | solution.py:548
  74.7 0.7 copy-start.5
  74.7 0.8 copy-start.6
  133.9 5.4 %copy-start.11 = (f32[256,256]{1,0:T(8,128)S(1)}, f32[256,256]{1,0:T(8,128)}, u32[]{:S(2)}) copy-start(f32[256,256]{1,0:T(8,128)} %get-tuple-element.34) | copy-start | bytes 786436
  133.9 6.9 %copy-start.10 = (f32[256,256]{1,0:T(8,128)S(1)}, f32[256,256]{1,0:T(8,128)}, u32[]{:S(2)}) copy-start(f32[256,256]{1,0:T(8,128)} %get-tuple-element.35) | copy-start | bytes 786436
  133.9 60.5 %all-to-all-start.3 = ((bf16[128,64,256]{2,1,0:T(8,128)(2,1)}), bf16[128,64,256]{2,1,0:T(8,128)(2,1)}, u32[]{:S(2)}, u32[]{:S(2)}) async-start(bf16[128,64,256]{2,1,0:T(8,128)(2,1)} %get-tuple-element.31), calls=%async_computation.3 | async-start | bytes 8388608 | tf_op jit(solution)/shard_map/all_to_all | solution.py:541
  139.4 55.0 %collective-permute-start.2 = (f32[256,256]{1,0:T(8,128)S(1)}, f32[256,256]{1,0:T(8,128)S(1)}, u32[]{:S(2)}, u32[]{:S(2)}) collective-permute-start(f32[256,256]{1,0:T(8,128)S(1)} %copy-done.11), channel_id=1, source_target_pairs={{0,1},{1,2},{2,3},{3,4},{4,5},{5,6},{6,7},{7,8},{8,9},{9,10},{10,1... | collective-permute-start | bytes 786440 | tf_op jit(solution)/shard_map/ppermute | solution.py:548
  140.8 53.6 %collective-permute-start.3 = (f32[256,256]{1,0:T(8,128)S(1)}, f32[256,256]{1,0:T(8,128)S(1)}, u32[]{:S(2)}, u32[]{:S(2)}) collective-permute-start(f32[256,256]{1,0:T(8,128)S(1)} %copy-done.10), channel_id=1, source_target_pairs={{1,0},{2,1},{3,2},{4,3},{5,4},{6,5},{7,6},{8,7},{9,8},{10,9},{11,1... | collective-permute-start | bytes 786440 | tf_op jit(solution)/shard_map/ppermute | solution.py:548
  154.5 0.6 copy-start.3
  155.1 0.7 copy-start.4
  194.4 0.7 copy-start.8
  194.4 0.8 copy-start.9
  253.7 9.8 %copy-start = (f32[4096,256]{1,0:T(8,128)S(1)}, f32[4096,256]{1,0:T(8,128)}, u32[]{:S(2)}) copy-start(f32[4096,256]{1,0:T(8,128)} %get-tuple-element.30.r) | copy-start | bytes 12582916
  253.7 9.8 %copy-start.1 = (f32[4096,256]{1,0:T(8,128)S(1)}, f32[4096,256]{1,0:T(8,128)}, u32[]{:S(2)}) copy-start(f32[4096,256]{1,0:T(8,128)} %get-tuple-element.29.sol) | copy-start | bytes 12582916
  253.7 9.8 %copy-start.2 = (f32[4096,256]{1,0:T(8,128)S(1)}, f32[4096,256]{1,0:T(8,128)}, u32[]{:S(2)}) copy-start(f32[4096,256]{1,0:T(8,128)} %get-tuple-element.36.image) | copy-start | bytes 12582916
